TPU v7x, 32 devices: a whole 2x2x4 slice. The times are simulated.
32 devices in a mesh: grp: 2 (over core), tab: 16 (over z, y, x).
Axes of the slice: x: 2, y: 2, z: 4, core: 2. Of those that a mesh axis runs over, the one named last changes fastest.
Arguments:
- sample_ids: int32 [4, 1024, 1024], P(None, ('grp', 'tab')), may hold values from 0 to 1535
- id_weights: bfloat16 [4, 1024, 1024], P(None, ('grp', 'tab')), may hold values from 0.25 to 2
- dense_features: bfloat16 [4, 1024, 128], P(None, ('grp', 'tab')), may hold values from -6 to 6
- click_labels: int32 [4, 1024], P(None, ('grp', 'tab')), may hold values 0 or 1
- table_shards: bfloat16 [128, 1536, 128], P('tab'), may hold values from -1.1953125 to 1.1953125
- slot_table: int32 [128], replicated, may hold values from 0 to 127, each once
- top_weight: bfloat16 [128, 1024], replicated, may hold values from -0.5 to 0.5
- top_bias: float32 [1024], replicated, may hold values from -3 to 3
- out_weight: bfloat16 [1024], replicated, may hold values from -0.1875 to 0.1875
Outputs:
- logits: float32 [4, 1024], P(None, ('grp', 'tab'))
- grad_top: float32 [128, 1024], replicated
- grad_bias: float32 [1024], replicated
Inputs may be any that keep to these rules, and one draw needn't show every extreme that they name: `slot_table`: a permutation: each table stands in exactly one slot.
All inputs are finite; a program needn't handle non-finite values. No bound on the sum of `click_labels` on one device may be relied on, other than what follows from the above.
Results may differ from a plain program's by a relative error of at most 0.0056.
Values may be sent and summed in bfloat16 or wider, within the bound.
A program may use at most 128 MiB of HBM per device.

v0:
```python
import functools
import math

import jax
import jax.numpy as jnp
from jax import lax
from jax.experimental import pallas as pl
from jax.experimental.pallas import tpu as pltpu
from jax.sharding import PartitionSpec as P

HOTS = 8
LANES = 128
loss_scale = 32768.0
NT = (((1,), (1,)), ((), ()))
MESH = pl.DeviceIdType.MESH
TN = (((0,), (0,)), ((), ()))


def column_of(row):
    size = row.shape[1]
    eye = lax.broadcasted_iota(jnp.int32, (size, size), 0) == lax.broadcasted_iota(jnp.int32, (size, size), 1)
    return jnp.sum(jnp.where(eye, row, 0.0), axis=1, keepdims=True)


def row_of(column):
    size = column.shape[0]
    eye = lax.broadcasted_iota(jnp.int32, (size, size), 0) == lax.broadcasted_iota(jnp.int32, (size, size), 1)
    return jnp.sum(jnp.where(eye, column, 0.0), axis=0, keepdims=True)


def step_kernel(count, groups, members, id_ref, weight_ref, source_ref, d_ref, t_ref, place_ref, label_ref, w_ref, b_ref, o_ref,
                logit_ref, top_ref, bias_ref,
                turned_ref, x_ref, pair_ref, fin_ref, xs_ref, ds_ref, lo_ref, key_ref, acc_ref, even_ref, odd_ref, mine_ref,
                got_ref, grad_ref, slope_ref, group_ref, half_ref, part_ref, bias_part,
                x_send, x_recv, d_send, d_recv, s_send, s_recv, g_send, g_recv, p_send, p_recv,
                b_send, b_recv, a_send, a_recv, f_send, f_recv, c_send, c_recv):
    my_g, my_t = lax.axis_index("grp"), lax.axis_index("tab")
    slots, vocab, width = t_ref.shape
    samples = x_ref.shape[1]
    blocks = vocab // LANES
    half = x_ref.shape[2] // 2
    hots = half // slots
    tables = got_ref.shape[0]
    hidden = w_ref.shape[1]
    piece = hidden // groups
    per = 2 if members % 2 == 0 else 1
    chunk = per * samples
    tile = 8

    def member(k):
        return lax.rem(my_t + k, members)

    def origin(k):
        return lax.rem(my_t - k + members, members)

    def team(k):
        return lax.rem(my_g + k, groups)

    def team_origin(k):
        return lax.rem(my_g - k + groups, groups)

    def remote(src, dst, send, recv, g, t):
        return pltpu.make_async_remote_copy(src_ref=src, dst_ref=dst, send_sem=send, recv_sem=recv,
                                            device_id={"grp": g, "tab": t}, device_id_type=MESH)

    def rows_of(t):
        return pl.ds(pl.multiple_of(t * slots, slots), slots)

    def cols_of(g):
        return pl.ds(pl.multiple_of(g * piece, LANES), piece)

    barrier = pltpu.get_barrier_semaphore()

    @pl.loop(1, members)
    def _(k):
        pl.semaphore_signal(barrier, inc=1, device_id={"grp": my_g, "tab": member(k)}, device_id_type=MESH)

    @pl.loop(1, groups)
    def _(k):
        pl.semaphore_signal(barrier, inc=1, device_id={"grp": team(k), "tab": my_t}, device_id_type=MESH)

    columns = id_ref.shape[2]
    ids = id_ref[...].reshape(samples, columns)
    code = jnp.left_shift(LANES + (ids & (LANES - 1)), jnp.right_shift(ids, LANES.bit_length() - 1))
    pair_ref[:, 0:columns] = code.astype(jnp.float32).astype(jnp.bfloat16)
    pair_ref[:, columns : 2 * columns] = weight_ref[...].reshape(samples, columns)

    @pl.loop(0, members)
    def _(m):
        spot = lax.broadcasted_iota(jnp.int32, (2 * columns, 2 * half), 0)
        chosen = (spot == source_ref[m]).astype(jnp.float32).astype(jnp.bfloat16)
        x_ref[m] = jnp.dot(pair_ref[...], chosen, preferred_element_type=jnp.float32).astype(jnp.bfloat16)

    pl.semaphore_wait(barrier, members + groups - 2)

    def x_copy(k):
        return remote(x_ref.at[member(k)], xs_ref.at[k], x_send.at[k], x_recv.at[k], my_g, member(k))

    def d_copy(k):
        return remote(d_ref, ds_ref.at[k], d_send.at[k], d_recv.at[k], my_g, member(k))

    def s_copy(k):
        return remote(mine_ref.at[k], got_ref.at[rows_of(my_t), :], s_send.at[k], s_recv.at[k], my_g, origin(k))

    @pl.loop(1, members)
    def _(k):
        d_copy(k).start()
        x_copy(k).start()

    xs_ref[0] = x_ref[my_t]
    ds_ref[0] = d_ref[...]

    @pl.loop(0, slots)
    def _(slot):
        turned_ref[slot] = t_ref[slot].T

    pick_row = lax.broadcasted_iota(jnp.int32, (slots, 2 * half), 0)
    pick_lane = lax.broadcasted_iota(jnp.int32, (slots, 2 * half), 1)
    choose = (pick_lane // hots == pick_row).astype(jnp.float32)

    @pl.loop(0, members // per)
    def _(i):
        for e in range(per):
            @pl.when(per * i + e > 0)
            def _():
                d_copy(per * i + e).wait_recv()
                x_copy(per * i + e).wait_recv()

        for e in range(per):
            at = pl.ds(e * samples, samples)
            code = xs_ref[per * i + e].astype(jnp.float32)
            lane = lax.broadcasted_iota(jnp.int32, code.shape, 1)
            high = jnp.zeros(code.shape, jnp.int32)
            for k in range(1, blocks):
                high = high + (code >= float(LANES << k)).astype(jnp.int32)
            lo_ref[at, :] = jnp.right_shift(code.astype(jnp.int32), high) & (LANES - 1)
            key_ref[at, :] = jnp.where(lane < half, (lane // hots) * blocks + high, -1)
            acc_ref[at, :] = jnp.zeros(code.shape, jnp.float32)

        def multiply(slot, g_ref):
            feats = ds_ref[pl.ds(per * i, per)].reshape(chunk, width)
            step = 2 * LANES if vocab % (2 * LANES) == 0 else LANES
            for p in range(vocab // step):
                g_ref[:, p * step : (p + 1) * step] = jnp.dot(
                    feats, turned_ref[slot, :, p * step : (p + 1) * step], preferred_element_type=jnp.float32)

        def pick(slot, g_ref):
            for r in range(chunk // tile):
                at = pl.ds(r * tile, tile)
                low = lo_ref[at, :]
                key = key_ref[at, :] - slot * blocks
                acc = acc_ref[at, :]
                for a in range(blocks):
                    part = g_ref[r * tile : (r + 1) * tile, a * LANES : (a + 1) * LANES]
                    got = jnp.take_along_axis(part, low, axis=1, mode="promise_in_bounds")
                    acc = jnp.where(key == a, got, acc)
                acc_ref[at, :] = acc

        multiply(0, even_ref)

        @pl.loop(0, slots // 2)
        def _(p):
            multiply(2 * p + 1, odd_ref)
            pick(2 * p, even_ref)
            multiply(jnp.minimum(2 * p + 2, slots - 1), even_ref)
            pick(2 * p + 1, odd_ref)

        for e in range(per):
            w = pltpu.roll(xs_ref[per * i + e].astype(jnp.float32), half, 1)
            lane = lax.broadcasted_iota(jnp.int32, w.shape, 1)
            prod = jnp.where(lane < half, acc_ref[e * samples : (e + 1) * samples, :] * w, 0.0)
            total = lax.dot_general(choose, prod, NT, preferred_element_type=jnp.float32,
                                    precision=lax.Precision.HIGHEST)
            mine_ref[per * i + e] = (total * (1.0 / math.sqrt(width))).astype(jnp.bfloat16).astype(jnp.float32)

        for e in range(per):
            @pl.when(per * i + e > 0)
            def _():
                s_copy(per * i + e).start()

    got_ref[rows_of(my_t), :] = mine_ref[0]

    @pl.loop(1, members)
    def _(k):
        d_copy(k).wait_send()
        x_copy(k).wait_send()
        s_copy(k).wait()

    row = lax.broadcasted_iota(jnp.int32, (tables, tables), 0)
    placed = (place_ref[...] == row).astype(jnp.bfloat16)
    scores = jnp.dot(placed, got_ref[...].astype(jnp.bfloat16), preferred_element_type=jnp.float32)
    scores = scores.astype(jnp.bfloat16)
    pre = lax.dot_general(scores, w_ref[...], TN, preferred_element_type=jnp.float32) + b_ref[...]
    gate = jax.nn.sigmoid(pre)
    value = (pre * gate).astype(jnp.bfloat16).astype(jnp.float32)
    out = o_ref[...].astype(jnp.float32)
    logit = jnp.sum(value * out, axis=1, keepdims=True)
    logit_row = row_of(logit)
    micro, local = logit_ref.shape
    for m in range(micro):
        logit_ref[m : m + 1, :] = logit_row[:, m * local : (m + 1) * local]
    labels = jnp.concatenate([label_ref[m : m + 1, :].astype(jnp.float32) for m in range(micro)], axis=1)
    delta = (jax.nn.sigmoid(logit) - column_of(labels)) * (loss_scale / count)
    slope = gate * (1.0 + pre * (1.0 - gate))
    slope_ref[...] = (delta * out * slope).astype(jnp.bfloat16)
    grad = slope_ref[...]
    grad_ref[pl.ds(tables, 8), :] = jnp.broadcast_to(
        jnp.sum(grad.astype(jnp.float32), axis=0, keepdims=True), (8, hidden))
    grad_ref[pl.ds(0, tables), :] = jnp.dot(scores, grad, preferred_element_type=jnp.float32)

    def g_copy(k):
        return remote(grad_ref.at[:, cols_of(team(k))], group_ref.at[k], g_send.at[k], g_recv.at[k], team(k), my_t)

    @pl.loop(1, groups)
    def _(k):
        g_copy(k).start()

    half_ref[...] = grad_ref[:, cols_of(my_g)]

    @pl.loop(1, groups)
    def _(k):
        g_copy(k).wait()
        half_ref[...] += group_ref[k]

    def p_copy(k):
        return remote(half_ref.at[rows_of(member(k)), :], part_ref.at[k], p_send.at[k], p_recv.at[k], my_g, member(k))

    def b_copy(k):
        return remote(half_ref.at[pl.ds(tables, 1), :], bias_part.at[k], b_send.at[k], b_recv.at[k], my_g, member(k))

    @pl.loop(1, members)
    def _(k):
        p_copy(k).start()

    @pl.loop(1, members)
    def _(k):
        b_copy(k).start()

    part_ref[0] = half_ref[rows_of(my_t), :]
    bias_part[0] = half_ref[tables : tables + 1, :]

    @pl.loop(1, members)
    def _(k):
        p_copy(k).wait()

    fin_ref[my_t, :, cols_of(my_g)] = jnp.sum(part_ref[...], axis=0).astype(jnp.bfloat16)

    def a_copy(k):
        at = fin_ref.at[my_t, :, cols_of(my_g)]
        return remote(at, at, a_send.at[k], a_recv.at[k], my_g, member(k))

    def f_copy(k, j):
        at = fin_ref.at[origin(k), :, cols_of(my_g)]
        return remote(at, at, f_send.at[j, k], f_recv.at[j, k], team(j), my_t)

    def c_copy(j):
        at = bias_ref.at[:, cols_of(my_g)]
        return remote(at, at, c_send.at[j], c_recv.at[j], team(j), my_t)

    @pl.loop(1, members)
    def _(k):
        a_copy(k).start()

    @pl.loop(1, groups)
    def _(j):
        f_copy(0, j).start()

    @pl.loop(1, members)
    def _(k):
        b_copy(k).wait()

    def add(q, total):
        return total + bias_part[lax.rem(my_t - q + members, members)]

    bias_ref[:, cols_of(my_g)] = lax.fori_loop(1, members, add, bias_part[my_t])

    @pl.loop(1, groups)
    def _(j):
        c_copy(j).start()

    @pl.loop(1, members)
    def _(k):
        a_copy(k).wait_recv()

        @pl.loop(1, groups)
        def _(j):
            f_copy(k, j).start()

    @pl.loop(1, members)
    def _(k):
        a_copy(k).wait_send()

    @pl.loop(1, groups)
    def _(j):
        c_copy(j).wait()

        @pl.loop(0, members)
        def _(k):
            f_copy(k, j).wait()

    for m in range(members):
        top_ref[m * slots : (m + 1) * slots, :] = fin_ref[m].astype(jnp.float32)


def fused_step(count, groups, members, ids, id_weights, source, d, table, slot_table, labels, weight, bias, out):
    samples, width = d.shape
    slots, vocab, _ = table.shape
    tables, hidden = weight.shape
    piece = hidden // groups
    chunk = samples * (2 if members % 2 == 0 else 1)
    lanes = source.shape[2]
    columns = ids.shape[2]
    vmem = pl.BlockSpec(memory_space=pltpu.VMEM)
    f32, bf16 = jnp.float32, jnp.bfloat16
    dma = pltpu.SemaphoreType.DMA
    return pl.pallas_call(
        functools.partial(step_kernel, count, groups, members),
        out_shape=(
            jax.ShapeDtypeStruct(labels.shape, f32),
            jax.ShapeDtypeStruct((tables, hidden), f32),
            jax.ShapeDtypeStruct((1, hidden), f32),
        ),
        in_specs=[vmem] * 10,
        out_specs=(vmem,) * 3,
        scratch_shapes=[
            pltpu.VMEM((slots, width, vocab), bf16),
            pltpu.VMEM((members, samples, lanes), bf16),
            pltpu.VMEM((samples, 2 * columns), bf16),
            pltpu.VMEM((members, slots, hidden), bf16),
            pltpu.VMEM((members, samples, lanes), bf16),
            pltpu.VMEM((members, samples, width), bf16),
            pltpu.VMEM((chunk, lanes), jnp.int32),
            pltpu.VMEM((chunk, lanes), jnp.int32),
            pltpu.VMEM((chunk, lanes), f32),
            pltpu.VMEM((chunk, vocab), f32),
            pltpu.VMEM((chunk, vocab), f32),
            pltpu.VMEM((members, slots, samples), f32),
            pltpu.VMEM((tables, samples), f32),
            pltpu.VMEM((tables + 8, hidden), f32),
            pltpu.VMEM((samples, hidden), bf16),
            pltpu.VMEM((groups, tables + 8, piece), f32),
            pltpu.VMEM((tables + 8, piece), f32),
            pltpu.VMEM((members, slots, piece), f32),
            pltpu.VMEM((members, 1, piece), f32),
        ]
        + [dma((members,))] * 6 + [dma((groups,))] * 2 + [dma((members,))] * 6
        + [dma((groups, members))] * 2 + [dma((groups,))] * 2,
        compiler_params=pltpu.CompilerParams(collective_id=1, has_side_effects=True),
    )(ids, id_weights, source, d, table, slot_table.reshape(1, -1), labels, weight, bias.reshape(1, -1), out.reshape(1, -1))


def per_device(
    sample_ids, id_weights, dense_features, click_labels, table_shards, slot_table, top_weight, top_bias, out_weight
):
    micro, local_batch, columns = sample_ids.shape
    tables = slot_table.shape[0]
    slots = table_shards.shape[0]
    width = dense_features.shape[2]
    hidden = top_weight.shape[1]
    members = lax.axis_size("tab")
    groups = lax.axis_size("grp")
    samples = micro * local_batch
    count = samples * groups * members
    hots = columns // tables
    own = slots * hots

    source = slot_table.reshape(members, slots, 1) * hots + jnp.arange(hots, dtype=jnp.int32)
    source = source.reshape(members, 1, own)
    source = jnp.concatenate([source, source + columns], axis=2)
    logit, grad_top, grad_bias = fused_step(
        count, groups, members, sample_ids, id_weights, source, dense_features.reshape(samples, width), table_shards,
        slot_table, click_labels, top_weight, top_bias, out_weight
    )
    return (logit, grad_top, grad_bias.reshape(hidden))


def solution(mesh):
    return jax.shard_map(
        per_device,
        mesh=mesh,
        in_specs=(
            P(None, ("grp", "tab"), None),
            P(None, ("grp", "tab"), None),
            P(None, ("grp", "tab"), None),
            P(None, ("grp", "tab")),
            P("tab", None, None),
            P(),
            P(),
            P(),
            P(),
        ),
        out_specs=(P(None, ("grp", "tab")), P(), P()),
        check_vma=False,
    )
```

profile of v0, /device:TPU:0, one launch (start us, length us, event | category | flops | bytes accessed | tf_op | source)
XLA Modules:
  0.0 92.8 jit_solution(1920211019410053029)
XLA Ops:
  0.6 0.7 broadcast_multiply_fusion
  1.3 1.3 %reshape.108.o_ref = bf16[1,1024]{1,0:T(2,128)(2,1)} reshape(bf16[1024]{0:T(1024)(128)(2,1)} %param.17) | data formatting | bytes 4096 | tf_op jit(solution)/shard_map/reshape | solution.py:349
  2.6 0.1 add.48
  2.7 0.1 mul.16
  2.7 0.1 copy.14
  2.8 0.1 copy.15
  2.9 0.7 pad_add_fusion.source_ref
  3.6 84.8 %shard_map.112 = (f32[4,32]{1,0:T(4,128)}, f32[128,1024]{1,0:T(8,128)}, f32[1,1024]{1,0:T(1,128)}) custom-call(s32[4,32,1024]{2,1,0:T(8,128)} %id_ref.1, bf16[4,32,1024]{2,1,0:T(8,128)(2,1)} %weight_ref.1, s32[16,1,128]{2,1,0:T(1,128)} %pad_add_fusion.source_ref, bf16[128,128]{1,0:T(8,128)(2,1)} %bitcast.7, bf16[8,1536,128]{2,1,0:T(8,128)(2,1)} %t_ref.1, ...), custom_call_target="tpu_custom_call" | custom-call | tf_op jit(solution)/shard_map/pallas_call | solution.py:316
  88.4 1.2 %copy.20 = f32[4,32]{1,0:T(4,128)} copy(f32[4,32]{1,0:T(4,128)} %get-tuple-element.14) | data formatting | bytes 1024
  89.7 1.9 %copy.21 = f32[128,1024]{1,0:T(8,128)} copy(f32[128,1024]{1,0:T(8,128)} %get-tuple-element.15) | data formatting | bytes 1048576
  91.6 1.3 %copy.22 = f32[1024]{0:T(1024)} copy(f32[1024]{0:T(1024)} %bitcast.9) | data formatting | bytes 8192
  (4 shorter events, 0.0 us)
where the time goes:
time: 93.1 us; the launch traced here: 92.8 us
  Pallas kernels  84.8 us (91%)
  local copies, waits for them, and re-layouts  5.99 us (6%)
  other arithmetic  1.38 us (1%)
    pallas_call x1, Pallas kernels, fused_step(): pl.pallas_call(functools.partial(step_kernel, count, groups, members), ou...  84.8 us
    unnamed x3, local copies, waits for them, and re-layouts  4.4 us

commit v1 on v0

--- a/solution.py
+++ b/solution.py
@@ -10,6 +10,7 @@
 
 HOTS = 8
 LANES = 128
+ROWS = 8
 loss_scale = 32768.0
 NT = (((1,), (1,)), ((), ()))
 MESH = pl.DeviceIdType.MESH
@@ -22,30 +23,46 @@
     return jnp.sum(jnp.where(eye, row, 0.0), axis=1, keepdims=True)
 
 
+def pick_rows(block, spot):
+    pick = lax.GatherDimensionNumbers(
+        offset_dims=(), collapsed_slice_dims=(0,), start_index_map=(0,),
+        operand_batching_dims=(1,), start_indices_batching_dims=(1,))
+    return lax.gather(block, spot[..., None], pick, (1, 1), mode=lax.GatherScatterMode.PROMISE_IN_BOUNDS)
+
+
+def choose_rows(tile_of, spot, bits, first, count):
+    if count == 1:
+        return pick_rows(tile_of(first), spot)
+    half = 1 << ((count - 1).bit_length() - 1)
+    low = choose_rows(tile_of, spot, bits, first, half)
+    high = choose_rows(tile_of, spot, bits, first + half, count - half)
+    return jnp.where(bits[half.bit_length() - 1], high, low)
+
+
 def row_of(column):
     size = column.shape[0]
     eye = lax.broadcasted_iota(jnp.int32, (size, size), 0) == lax.broadcasted_iota(jnp.int32, (size, size), 1)
     return jnp.sum(jnp.where(eye, column, 0.0), axis=0, keepdims=True)
 
 
-def step_kernel(count, groups, members, id_ref, weight_ref, source_ref, d_ref, t_ref, place_ref, label_ref, w_ref, b_ref, o_ref,
+def step_kernel(count, groups, members, id_ref, weight_ref, table_ref, d_ref, t_ref, place_ref, label_ref, w_ref, b_ref, o_ref,
                 logit_ref, top_ref, bias_ref,
-                turned_ref, x_ref, pair_ref, fin_ref, xs_ref, ds_ref, lo_ref, key_ref, acc_ref, even_ref, odd_ref, mine_ref,
+                code_ref, turned_ref, x_ref, fin_ref, xs_ref, ds_ref, key_ref, scale_ref, acc_ref, mine_ref,
                 got_ref, grad_ref, slope_ref, group_ref, half_ref, part_ref, bias_part,
                 x_send, x_recv, d_send, d_recv, s_send, s_recv, g_send, g_recv, p_send, p_recv,
                 b_send, b_recv, a_send, a_recv, f_send, f_recv, c_send, c_recv):
     my_g, my_t = lax.axis_index("grp"), lax.axis_index("tab")
     slots, vocab, width = t_ref.shape
-    samples = x_ref.shape[1]
+    own = x_ref.shape[1] // 2
+    samples = x_ref.shape[2]
+    hots = own // slots
     blocks = vocab // LANES
-    half = x_ref.shape[2] // 2
-    hots = half // slots
+    tiles = vocab // ROWS
     tables = got_ref.shape[0]
     hidden = w_ref.shape[1]
     piece = hidden // groups
     per = 2 if members % 2 == 0 else 1
     chunk = per * samples
-    tile = 8
 
     def member(k):
         return lax.rem(my_t + k, members)
@@ -80,16 +97,21 @@
         pl.semaphore_signal(barrier, inc=1, device_id={"grp": team(k), "tab": my_t}, device_id_type=MESH)
 
     columns = id_ref.shape[2]
-    ids = id_ref[...].reshape(samples, columns)
-    code = jnp.left_shift(LANES + (ids & (LANES - 1)), jnp.right_shift(ids, LANES.bit_length() - 1))
-    pair_ref[:, 0:columns] = code.astype(jnp.float32).astype(jnp.bfloat16)
-    pair_ref[:, columns : 2 * columns] = weight_ref[...].reshape(samples, columns)
+    step = LANES // hots
+    for c in range(columns // LANES):
+        at = slice(c * LANES, (c + 1) * LANES)
+        ids = id_ref[:, :, at].reshape(samples, LANES)
+        code = jnp.left_shift(LANES + (ids & (LANES - 1)), jnp.right_shift(ids, LANES.bit_length() - 1))
+        code = code.astype(jnp.float32).astype(jnp.bfloat16)
+        code_ref[c * step : (c + 1) * step] = code.T.astype(jnp.float32).reshape(step, hots, samples)
+        share = weight_ref[:, :, at].reshape(samples, LANES)
+        turned_ref[c * step : (c + 1) * step] = share.T.astype(jnp.float32).reshape(step, hots, samples)
 
     @pl.loop(0, members)
     def _(m):
-        spot = lax.broadcasted_iota(jnp.int32, (2 * columns, 2 * half), 0)
-        chosen = (spot == source_ref[m]).astype(jnp.float32).astype(jnp.bfloat16)
-        x_ref[m] = jnp.dot(pair_ref[...], chosen, preferred_element_type=jnp.float32).astype(jnp.bfloat16)
+        held = [table_ref[m * slots + s] for s in range(slots)]
+        x_ref[m, 0:own] = jnp.concatenate([code_ref[t] for t in held], axis=0).astype(jnp.bfloat16)
+        x_ref[m, own : 2 * own] = jnp.concatenate([turned_ref[t] for t in held], axis=0).astype(jnp.bfloat16)
 
     pl.semaphore_wait(barrier, members + groups - 2)
 
@@ -110,13 +132,8 @@
     xs_ref[0] = x_ref[my_t]
     ds_ref[0] = d_ref[...]
 
-    @pl.loop(0, slots)
-    def _(slot):
-        turned_ref[slot] = t_ref[slot].T
-
-    pick_row = lax.broadcasted_iota(jnp.int32, (slots, 2 * half), 0)
-    pick_lane = lax.broadcasted_iota(jnp.int32, (slots, 2 * half), 1)
-    choose = (pick_lane // hots == pick_row).astype(jnp.float32)
+    parts = 2 if vocab % (2 * ROWS) == 0 else 1
+    unroll = 4 if slots % 4 == 0 else 1
 
     @pl.loop(0, members // per)
     def _(i):
@@ -127,50 +144,39 @@
                 x_copy(per * i + e).wait_recv()
 
         for e in range(per):
-            at = pl.ds(e * samples, samples)
-            code = xs_ref[per * i + e].astype(jnp.float32)
-            lane = lax.broadcasted_iota(jnp.int32, code.shape, 1)
+            code = xs_ref[per * i + e, 0:own].astype(jnp.float32)
             high = jnp.zeros(code.shape, jnp.int32)
             for k in range(1, blocks):
                 high = high + (code >= float(LANES << k)).astype(jnp.int32)
-            lo_ref[at, :] = jnp.right_shift(code.astype(jnp.int32), high) & (LANES - 1)
-            key_ref[at, :] = jnp.where(lane < half, (lane // hots) * blocks + high, -1)
-            acc_ref[at, :] = jnp.zeros(code.shape, jnp.float32)
-
-        def multiply(slot, g_ref):
+            low = jnp.right_shift(code.astype(jnp.int32), high) & (LANES - 1)
+            key_ref[e] = high * LANES + low
+            scale_ref[e] = xs_ref[per * i + e, own : 2 * own].astype(jnp.float32)
+
+        def look(slot):
             feats = ds_ref[pl.ds(per * i, per)].reshape(chunk, width)
-            step = 2 * LANES if vocab % (2 * LANES) == 0 else LANES
-            for p in range(vocab // step):
-                g_ref[:, p * step : (p + 1) * step] = jnp.dot(
-                    feats, turned_ref[slot, :, p * step : (p + 1) * step], preferred_element_type=jnp.float32)
-
-        def pick(slot, g_ref):
-            for r in range(chunk // tile):
-                at = pl.ds(r * tile, tile)
-                low = lo_ref[at, :]
-                key = key_ref[at, :] - slot * blocks
-                acc = acc_ref[at, :]
-                for a in range(blocks):
-                    part = g_ref[r * tile : (r + 1) * tile, a * LANES : (a + 1) * LANES]
-                    got = jnp.take_along_axis(part, low, axis=1, mode="promise_in_bounds")
-                    acc = jnp.where(key == a, got, acc)
-                acc_ref[at, :] = acc
-
-        multiply(0, even_ref)
-
-        @pl.loop(0, slots // 2)
-        def _(p):
-            multiply(2 * p + 1, odd_ref)
-            pick(2 * p, even_ref)
-            multiply(jnp.minimum(2 * p + 2, slots - 1), even_ref)
-            pick(2 * p + 1, odd_ref)
+            size = vocab // parts
+            products = [lax.dot_general(t_ref[slot, p * size : (p + 1) * size, :], feats, NT,
+                                        preferred_element_type=jnp.float32) for p in range(parts)]
+            at = pl.ds(pl.multiple_of(slot * hots, hots), hots)
+            for e in range(per):
+                key = key_ref[e, at, :]
+                high = jnp.right_shift(key, ROWS.bit_length() - 1)
+                bits = [(high & (1 << b)) != 0 for b in range((tiles - 1).bit_length())]
+
+                def tile_of(v, e=e):
+                    p, r = divmod(v * ROWS, size)
+                    return products[p][r : r + ROWS, e * samples : (e + 1) * samples]
+
+                got = choose_rows(tile_of, key & (ROWS - 1), bits, 0, tiles)
+                acc_ref[e, at, :] = got * scale_ref[e, at, :]
+
+        @pl.loop(0, slots // unroll)
+        def _(q):
+            for u in range(unroll):
+                look(q * unroll + u)
 
         for e in range(per):
-            w = pltpu.roll(xs_ref[per * i + e].astype(jnp.float32), half, 1)
-            lane = lax.broadcasted_iota(jnp.int32, w.shape, 1)
-            prod = jnp.where(lane < half, acc_ref[e * samples : (e + 1) * samples, :] * w, 0.0)
-            total = lax.dot_general(choose, prod, NT, preferred_element_type=jnp.float32,
-                                    precision=lax.Precision.HIGHEST)
+            total = jnp.sum(acc_ref[e].reshape(slots, hots, samples), axis=1)
             mine_ref[per * i + e] = (total * (1.0 / math.sqrt(width))).astype(jnp.bfloat16).astype(jnp.float32)
 
         for e in range(per):
@@ -302,15 +308,16 @@
         top_ref[m * slots : (m + 1) * slots, :] = fin_ref[m].astype(jnp.float32)
 
 
-def fused_step(count, groups, members, ids, id_weights, source, d, table, slot_table, labels, weight, bias, out):
+def fused_step(count, groups, members, ids, id_weights, d, table, slot_table, labels, weight, bias, out):
     samples, width = d.shape
     slots, vocab, _ = table.shape
     tables, hidden = weight.shape
     piece = hidden // groups
-    chunk = samples * (2 if members % 2 == 0 else 1)
-    lanes = source.shape[2]
-    columns = ids.shape[2]
+    per = 2 if members % 2 == 0 else 1
+    hots = ids.shape[2] // tables
+    own = slots * hots
     vmem = pl.BlockSpec(memory_space=pltpu.VMEM)
+    smem = pl.BlockSpec(memory_space=pltpu.SMEM)
     f32, bf16 = jnp.float32, jnp.bfloat16
     dma = pltpu.SemaphoreType.DMA
     return pl.pallas_call(
@@ -320,20 +327,18 @@
             jax.ShapeDtypeStruct((tables, hidden), f32),
             jax.ShapeDtypeStruct((1, hidden), f32),
         ),
-        in_specs=[vmem] * 10,
+        in_specs=[vmem] * 2 + [smem] + [vmem] * 7,
         out_specs=(vmem,) * 3,
         scratch_shapes=[
-            pltpu.VMEM((slots, width, vocab), bf16),
-            pltpu.VMEM((members, samples, lanes), bf16),
-            pltpu.VMEM((samples, 2 * columns), bf16),
+            pltpu.VMEM((tables, hots, samples), f32),
+            pltpu.VMEM((tables, hots, samples), f32),
+            pltpu.VMEM((members, 2 * own, samples), bf16),
             pltpu.VMEM((members, slots, hidden), bf16),
-            pltpu.VMEM((members, samples, lanes), bf16),
+            pltpu.VMEM((members, 2 * own, samples), bf16),
             pltpu.VMEM((members, samples, width), bf16),
-            pltpu.VMEM((chunk, lanes), jnp.int32),
-            pltpu.VMEM((chunk, lanes), jnp.int32),
-            pltpu.VMEM((chunk, lanes), f32),
-            pltpu.VMEM((chunk, vocab), f32),
-            pltpu.VMEM((chunk, vocab), f32),
+            pltpu.VMEM((per, own, samples), jnp.int32),
+            pltpu.VMEM((per, own, samples), f32),
+            pltpu.VMEM((per, own, samples), f32),
             pltpu.VMEM((members, slots, samples), f32),
             pltpu.VMEM((tables, samples), f32),
             pltpu.VMEM((tables + 8, hidden), f32),
@@ -346,7 +351,7 @@
         + [dma((members,))] * 6 + [dma((groups,))] * 2 + [dma((members,))] * 6
         + [dma((groups, members))] * 2 + [dma((groups,))] * 2,
         compiler_params=pltpu.CompilerParams(collective_id=1, has_side_effects=True),
-    )(ids, id_weights, source, d, table, slot_table.reshape(1, -1), labels, weight, bias.reshape(1, -1), out.reshape(1, -1))
+    )(ids, id_weights, slot_table, d, table, slot_table.reshape(1, -1), labels, weight, bias.reshape(1, -1), out.reshape(1, -1))
 
 
 def per_device(
@@ -361,14 +366,8 @@
     groups = lax.axis_size("grp")
     samples = micro * local_batch
     count = samples * groups * members
-    hots = columns // tables
-    own = slots * hots
-
-    source = slot_table.reshape(members, slots, 1) * hots + jnp.arange(hots, dtype=jnp.int32)
-    source = source.reshape(members, 1, own)
-    source = jnp.concatenate([source, source + columns], axis=2)
     logit, grad_top, grad_bias = fused_step(
-        count, groups, members, sample_ids, id_weights, source, dense_features.reshape(samples, width), table_shards,
+        count, groups, members, sample_ids, id_weights, dense_features.reshape(samples, width), table_shards,
         slot_table, click_labels, top_weight, top_bias, out_weight
     )
     return (logit, grad_top, grad_bias.reshape(hidden))

time: 93.1 us -> 72.9 us (0.78)
  Pallas kernels: 84.8 us -> 66.4 us
  other arithmetic: 1.38 us -> 0 us
    pallas_call x1, Pallas kernels: 84.8 us -> 66.4 us  [fused_step(): pl.pallas_call(functools.partial(step_kernel, count, groups, members), ou...]
where the time goes in v1:
time: 72.9 us; the launch traced here: 72.7 us
  Pallas kernels  66.4 us (91%)
  local copies, waits for them, and re-layouts  5.68 us (8%)
    pallas_call x1, Pallas kernels, fused_step(): pl.pallas_call(functools.partial(step_kernel, count, groups, members), ou...  66.4 us
    unnamed x3, local copies, waits for them, and re-layouts  4.4 us

profile of v1, /device:TPU:0, one launch (start us, length us, event | category | flops | bytes accessed | tf_op | source)
XLA Modules:
  0.0 72.7 jit_solution(10754576903914750265)
XLA Ops:
  0.6 1.3 %reshape.24.o_ref = bf16[1,1024]{1,0:T(2,128)(2,1)} reshape(bf16[1024]{0:T(1024)(128)(2,1)} %param.17) | data formatting | bytes 4096 | tf_op jit(solution)/shard_map/reshape | solution.py:354
  1.9 66.4 %shard_map.112 = (f32[4,32]{1,0:T(4,128)}, f32[128,1024]{1,0:T(8,128)}, f32[1,1024]{1,0:T(1,128)}) custom-call(s32[4,32,1024]{2,1,0:T(8,128)} %id_ref.1, bf16[4,32,1024]{2,1,0:T(8,128)(2,1)} %weight_ref.1, s32[128]{0:T(128)} %table_ref.1, bf16[128,128]{1,0:T(8,128)(2,1)} %bitcast.4, bf16[8,1536,128]{2,1,0:T(8,128)(2,1)} %t_ref.1, s32[1,128]{1,0:T(1,128)} %bitcast.7, ...), custom_call_target="tpu_custom_call" | custom-call | tf_op jit(solution)/shard_map/pallas_call | solution.py:323
  68.3 1.2 %copy.15 = f32[4,32]{1,0:T(4,128)} copy(f32[4,32]{1,0:T(4,128)} %get-tuple-element.12) | data formatting | bytes 1024
  69.6 1.9 %copy.16 = f32[128,1024]{1,0:T(8,128)} copy(f32[128,1024]{1,0:T(8,128)} %get-tuple-element.13) | data formatting | bytes 1048576
  71.4 1.3 %copy.17 = f32[1024]{0:T(1024)} copy(f32[1024]{0:T(1024)} %bitcast.5) | data formatting | bytes 8192

commit v2 on v1

--- a/solution.py
+++ b/solution.py
@@ -64,11 +64,24 @@
     per = 2 if members % 2 == 0 else 1
     chunk = per * samples
 
+    plane = max(n for n in range(1, members + 1) if members % n == 0 and n * n <= members)
+    lines = members // plane
+    even = members & (members - 1) == 0
+
+    def move(k, way):
+        if even:
+            spot = 0
+            for bit in range(members.bit_length() - 1):
+                spot = spot + lax.rem(lax.div(my_t, 1 << bit) + lax.div(k, 1 << bit), 2) * (1 << bit)
+            return spot
+        line = lax.rem(lax.div(my_t, plane) + way * lax.div(k, plane) + lines, lines)
+        return line * plane + lax.rem(lax.rem(my_t, plane) + way * lax.rem(k, plane) + plane, plane)
+
     def member(k):
-        return lax.rem(my_t + k, members)
+        return move(jnp.int32(k), 1)
 
     def origin(k):
-        return lax.rem(my_t - k + members, members)
+        return move(jnp.int32(k), -1)
 
     def team(k):
         return lax.rem(my_g + k, groups)
@@ -121,12 +134,30 @@
     def d_copy(k):
         return remote(d_ref, ds_ref.at[k], d_send.at[k], d_recv.at[k], my_g, member(k))
 
+    def pass_copy(line, k):
+        at = line * plane + k
+        return remote(ds_ref.at[line * plane], ds_ref.at[at], d_send.at[at], d_recv.at[at], my_g, member(k))
+
     def s_copy(k):
         return remote(mine_ref.at[k], got_ref.at[rows_of(my_t), :], s_send.at[k], s_recv.at[k], my_g, origin(k))
 
-    @pl.loop(1, members)
+    @pl.loop(1, lines)
+    def _(line):
+        d_copy(line * plane).start()
+
+    @pl.loop(1, plane)
     def _(k):
         d_copy(k).start()
+
+    for k in range(1, per):
+        x_copy(k).start()
+
+    @pl.loop(2 * per, members)
+    def _(k):
+        x_copy(k).start()
+
+    @pl.loop(per, min(2 * per, members))
+    def _(k):
         x_copy(k).start()
 
     xs_ref[0] = x_ref[my_t]
@@ -135,12 +166,29 @@
     parts = 2 if vocab % (2 * ROWS) == 0 else 1
     unroll = 4 if slots % 4 == 0 else 1
 
-    @pl.loop(0, members // per)
-    def _(i):
+    turns = members // per
+
+    @pl.loop(0, turns)
+    def _(turn):
+        @pl.when(turn == 1)
+        def _():
+            @pl.loop(1, lines)
+            def _(line):
+                d_copy(line * plane).wait_recv()
+
+                @pl.loop(1, plane)
+                def _(k):
+                    pass_copy(line, k).start()
+
+        i = lax.div(turn + turns - 2, turns - 1) * (1 + lax.rem(turn, turns - 1)) if turns > 1 else turn
+
         for e in range(per):
+            @pl.when(lax.rem(per * i + e, plane) > 0)
+            def _():
+                d_copy(per * i + e).wait_recv()
+
             @pl.when(per * i + e > 0)
             def _():
-                d_copy(per * i + e).wait_recv()
                 x_copy(per * i + e).wait_recv()
 
         for e in range(per):

time: 72.9 us -> 63.8 us (0.88)
  Pallas kernels: 66.4 us -> 57.3 us
    pallas_call x1, Pallas kernels: 66.4 us -> 57.3 us  [fused_step(): pl.pallas_call(functools.partial(step_kernel, count, groups, members), ou...]
where the time goes in v2:
time: 63.8 us; the launch traced here: 63.6 us
  Pallas kernels  57.3 us (90%)
  local copies, waits for them, and re-layouts  5.68 us (9%)
  between operations  0.64 us (1%)
    pallas_call x1, Pallas kernels, fused_step(): pl.pallas_call(functools.partial(step_kernel, count, groups, members), ou...  57.3 us
    unnamed x3, local copies, waits for them, and re-layouts  4.4 us
    reshape x1, local copies, waits for them, and re-layouts, fused_step(): out.reshape(1, -1)  1.28 us

profile of v2, /device:TPU:0, one launch (start us, length us, event | category | flops | bytes accessed | tf_op | source)
XLA Modules:
  0.0 63.6 jit_solution(201814971470051185)
XLA Ops:
  0.6 1.3 %reshape.24.o_ref = bf16[1,1024]{1,0:T(2,128)(2,1)} reshape(bf16[1024]{0:T(1024)(128)(2,1)} %param.17) | data formatting | bytes 4096 | tf_op jit(solution)/shard_map/reshape | solution.py:402
  1.9 57.3 %shard_map.112 = (f32[4,32]{1,0:T(4,128)}, f32[128,1024]{1,0:T(8,128)}, f32[1,1024]{1,0:T(1,128)}) custom-call(s32[4,32,1024]{2,1,0:T(8,128)} %id_ref.1, bf16[4,32,1024]{2,1,0:T(8,128)(2,1)} %weight_ref.1, s32[128]{0:T(128)} %table_ref.1, bf16[128,128]{1,0:T(8,128)(2,1)} %bitcast.4, bf16[8,1536,128]{2,1,0:T(8,128)(2,1)} %t_ref.1, s32[1,128]{1,0:T(1,128)} %bitcast.7, ...), custom_call_target="tpu_custom_call" | custom-call | tf_op jit(solution)/shard_map/pallas_call | solution.py:371
  59.2 1.2 %copy.15 = f32[4,32]{1,0:T(4,128)} copy(f32[4,32]{1,0:T(4,128)} %get-tuple-element.12) | data formatting | bytes 1024
  60.4 1.9 %copy.16 = f32[128,1024]{1,0:T(8,128)} copy(f32[128,1024]{1,0:T(8,128)} %get-tuple-element.13) | data formatting | bytes 1048576
  62.3 1.3 %copy.17 = f32[1024]{0:T(1024)} copy(f32[1024]{0:T(1024)} %bitcast.5) | data formatting | bytes 8192

commit v3 on v2

--- a/solution.py
+++ b/solution.py
@@ -45,14 +45,16 @@
     return jnp.sum(jnp.where(eye, column, 0.0), axis=0, keepdims=True)
 
 
-def step_kernel(count, groups, members, id_ref, weight_ref, table_ref, d_ref, t_ref, place_ref, label_ref, w_ref, b_ref, o_ref,
-                logit_ref, top_ref, bias_ref,
-                code_ref, turned_ref, x_ref, fin_ref, xs_ref, ds_ref, key_ref, scale_ref, acc_ref, mine_ref,
+def step_kernel(count, groups, members, ids, weights, table_of, feats_in, shards, place_in, labels_in, top_in, bias_in, out_in,
+                logit_out, top_out, bias_out,
+                id_ref, weight_ref, table_ref, t_ref, place_ref, label_ref, w_ref, b_ref, o_ref, logit_ref, bias_ref,
+                load_sem, store_sem, code_ref, turned_ref, x_ref, fin_ref, xs_ref, ds_ref, key_ref, scale_ref, acc_ref, mine_ref,
                 got_ref, grad_ref, slope_ref, group_ref, half_ref, part_ref, bias_part,
                 x_send, x_recv, d_send, d_recv, s_send, s_recv, g_send, g_recv, p_send, p_recv,
                 b_send, b_recv, a_send, a_recv, f_send, f_recv, c_send, c_recv):
     my_g, my_t = lax.axis_index("grp"), lax.axis_index("tab")
     slots, vocab, width = t_ref.shape
+    micro, local, columns = id_ref.shape
     own = x_ref.shape[1] // 2
     samples = x_ref.shape[2]
     hots = own // slots
@@ -109,7 +111,14 @@
     def _(k):
         pl.semaphore_signal(barrier, inc=1, device_id={"grp": team(k), "tab": my_t}, device_id_type=MESH)
 
-    columns = id_ref.shape[2]
+    loads = [pltpu.make_async_copy(src, dst, load_sem.at[n]) for n, (src, dst) in enumerate((
+        (table_of, table_ref), (ids, id_ref), (weights, weight_ref), (feats_in, ds_ref.at[0]), (shards, t_ref),
+        (place_in, place_ref), (labels_in, label_ref), (top_in, w_ref), (bias_in, b_ref), (out_in, o_ref)))]
+    for load in loads:
+        load.start()
+    for load in loads[:3]:
+        load.wait()
+
     step = LANES // hots
     for c in range(columns // LANES):
         at = slice(c * LANES, (c + 1) * LANES)
@@ -126,13 +135,14 @@
         x_ref[m, 0:own] = jnp.concatenate([code_ref[t] for t in held], axis=0).astype(jnp.bfloat16)
         x_ref[m, own : 2 * own] = jnp.concatenate([turned_ref[t] for t in held], axis=0).astype(jnp.bfloat16)
 
+    loads[3].wait()
     pl.semaphore_wait(barrier, members + groups - 2)
 
     def x_copy(k):
         return remote(x_ref.at[member(k)], xs_ref.at[k], x_send.at[k], x_recv.at[k], my_g, member(k))
 
     def d_copy(k):
-        return remote(d_ref, ds_ref.at[k], d_send.at[k], d_recv.at[k], my_g, member(k))
+        return remote(ds_ref.at[0], ds_ref.at[k], d_send.at[k], d_recv.at[k], my_g, member(k))
 
     def pass_copy(line, k):
         at = line * plane + k
@@ -161,7 +171,7 @@
         x_copy(k).start()
 
     xs_ref[0] = x_ref[my_t]
-    ds_ref[0] = d_ref[...]
+    loads[4].wait()
 
     parts = 2 if vocab % (2 * ROWS) == 0 else 1
     unroll = 4 if slots % 4 == 0 else 1
@@ -240,6 +250,8 @@
         x_copy(k).wait_send()
         s_copy(k).wait()
 
+    for load in loads[5:]:
+        load.wait()
     row = lax.broadcasted_iota(jnp.int32, (tables, tables), 0)
     placed = (place_ref[...] == row).astype(jnp.bfloat16)
     scores = jnp.dot(placed, got_ref[...].astype(jnp.bfloat16), preferred_element_type=jnp.float32)
@@ -248,11 +260,13 @@
     gate = jax.nn.sigmoid(pre)
     value = (pre * gate).astype(jnp.bfloat16).astype(jnp.float32)
     out = o_ref[...].astype(jnp.float32)
+    out = jnp.concatenate([out[r : r + 1, :] for r in range(out.shape[0])], axis=1)
     logit = jnp.sum(value * out, axis=1, keepdims=True)
     logit_row = row_of(logit)
-    micro, local = logit_ref.shape
     for m in range(micro):
         logit_ref[m : m + 1, :] = logit_row[:, m * local : (m + 1) * local]
+    logit_store = pltpu.make_async_copy(logit_ref, logit_out, store_sem.at[0])
+    logit_store.start()
     labels = jnp.concatenate([label_ref[m : m + 1, :].astype(jnp.float32) for m in range(micro)], axis=1)
     delta = (jax.nn.sigmoid(logit) - column_of(labels)) * (loss_scale / count)
     slope = gate * (1.0 + pre * (1.0 - gate))
@@ -352,8 +366,20 @@
         def _(k):
             f_copy(k, j).wait()
 
+    stores = [pltpu.make_async_copy(fin_ref, top_out, store_sem.at[1]),
+              pltpu.make_async_copy(bias_ref, bias_out, store_sem.at[2])]
+    for store in stores:
+        store.start()
+    for store in [logit_store] + stores:
+        store.wait()
+
+
+def finish_kernel(logit_in, top_in, bias_in, logit_ref, top_ref, bias_ref):
+    logit_ref[...] = logit_in[...]
+    members, slots, _ = top_in.shape
     for m in range(members):
-        top_ref[m * slots : (m + 1) * slots, :] = fin_ref[m].astype(jnp.float32)
+        top_ref[m * slots : (m + 1) * slots, :] = top_in[m].astype(jnp.float32)
+    bias_ref[...] = bias_in[...]
 
 
 def fused_step(count, groups, members, ids, id_weights, d, table, slot_table, labels, weight, bias, out):
@@ -365,19 +391,32 @@
     hots = ids.shape[2] // tables
     own = slots * hots
     vmem = pl.BlockSpec(memory_space=pltpu.VMEM)
-    smem = pl.BlockSpec(memory_space=pltpu.SMEM)
+    hbm = pl.BlockSpec(memory_space=pltpu.HBM)
     f32, bf16 = jnp.float32, jnp.bfloat16
     dma = pltpu.SemaphoreType.DMA
-    return pl.pallas_call(
+    logit, top, side = pl.pallas_call(
         functools.partial(step_kernel, count, groups, members),
         out_shape=(
             jax.ShapeDtypeStruct(labels.shape, f32),
-            jax.ShapeDtypeStruct((tables, hidden), f32),
+            jax.ShapeDtypeStruct((members, slots, hidden), bf16),
             jax.ShapeDtypeStruct((1, hidden), f32),
         ),
-        in_specs=[vmem] * 2 + [smem] + [vmem] * 7,
-        out_specs=(vmem,) * 3,
+        in_specs=[hbm] * 10,
+        out_specs=(hbm,) * 3,
         scratch_shapes=[
+            pltpu.VMEM(ids.shape, jnp.int32),
+            pltpu.VMEM(ids.shape, bf16),
+            pltpu.SMEM((tables,), jnp.int32),
+            pltpu.VMEM(table.shape, bf16),
+            pltpu.VMEM((1, tables), jnp.int32),
+            pltpu.VMEM(labels.shape, jnp.int32),
+            pltpu.VMEM(weight.shape, bf16),
+            pltpu.VMEM((1, hidden), f32),
+            pltpu.VMEM((hidden // LANES, LANES), bf16),
+            pltpu.VMEM(labels.shape, f32),
+            pltpu.VMEM((1, hidden), f32),
+            dma((10,)),
+            dma((3,)),
             pltpu.VMEM((tables, hots, samples), f32),
             pltpu.VMEM((tables, hots, samples), f32),
             pltpu.VMEM((members, 2 * own, samples), bf16),
@@ -399,7 +438,18 @@
         + [dma((members,))] * 6 + [dma((groups,))] * 2 + [dma((members,))] * 6
         + [dma((groups, members))] * 2 + [dma((groups,))] * 2,
         compiler_params=pltpu.CompilerParams(collective_id=1, has_side_effects=True),
-    )(ids, id_weights, slot_table, d, table, slot_table.reshape(1, -1), labels, weight, bias.reshape(1, -1), out.reshape(1, -1))
+    )(ids, id_weights, slot_table, d, table, slot_table.reshape(1, -1), labels, weight, bias.reshape(1, -1),
+      out.reshape(-1, LANES))
+    return pl.pallas_call(
+        finish_kernel,
+        out_shape=(
+            jax.ShapeDtypeStruct(labels.shape, f32),
+            jax.ShapeDtypeStruct((tables, hidden), f32),
+            jax.ShapeDtypeStruct((1, hidden), f32),
+        ),
+        in_specs=[vmem] * 3,
+        out_specs=(vmem,) * 3,
+    )(logit, top, side)
 
 
 def per_device(

time: 63.8 us -> 57.8 us (0.906)
  local copies, waits for them, and re-layouts: 5.68 us -> 0 us
    unnamed x3 -> x0, local copies, waits for them, and re-layouts: 4.4 us -> none
    pallas_call x1, Pallas kernels: 57.3 us -> 55.2 us  [fused_step(): pl.pallas_call(functools.partial(step_kernel, count, groups, members), ou...]
    pallas_call x0 -> x1, Pallas kernels: none -> 1.78 us  [fused_step(): pl.pallas_call(finish_kernel, out_shape=(jax.ShapeDtypeStruct(labels.shap...]
    reshape x1 -> x0, local copies, waits for them, and re-layouts: 1.28 us -> none  [fused_step(): out.reshape(1, -1)]
where the time goes in v3:
time: 57.8 us; the launch traced here: 57.6 us
  Pallas kernels  57 us (99%)
  between operations  0.64 us (1%)
    pallas_call x1, Pallas kernels, fused_step(): pl.pallas_call(functools.partial(step_kernel, count, groups, members), ou...  55.2 us
    pallas_call x1, Pallas kernels, fused_step(): pl.pallas_call(finish_kernel, out_shape=(jax.ShapeDtypeStruct(labels.shap...  1.78 us

profile of v3, /device:TPU:0, one launch (start us, length us, event | category | flops | bytes accessed | tf_op | source)
XLA Modules:
  0.0 57.6 jit_solution(8721107300998579402)
XLA Ops:
  0.6 55.2 %shard_map.112 = (f32[4,32]{1,0:T(4,128)}, bf16[16,8,1024]{2,1,0:T(8,128)(2,1)}, f32[1,1024]{1,0:T(1,128)}) custom-call(s32[4,32,1024]{2,1,0:T(8,128)} %ids.1, bf16[4,32,1024]{2,1,0:T(8,128)(2,1)} %weights.1, s32[128]{0:T(128)} %table_of.1, bf16[128,128]{1,0:T(8,128)(2,1)} %bitcast.5, bf16[8,1536,128]{2,1,0:T(8,128)(2,1)} %shards.1, s32[1,128]{1,0:T(1,128)} %bitcast.8, ...), custom_call_target="tpu_custom_call" | custom-call | tf_op jit(solution)/shard_map/pallas_call | solution.py:397
  55.9 1.8 %shard_map.113 = (f32[4,32]{1,0:T(4,128)}, f32[128,1024]{1,0:T(8,128)}, f32[1,1024]{1,0:T(1,128)}) custom-call(f32[4,32]{1,0:T(4,128)} %get-tuple-element.9.logit_in, bf16[16,8,1024]{2,1,0:T(8,128)(2,1)} %get-tuple-element.10.top_in, f32[1,1024]{1,0:T(1,128)} %get-tuple-element.11.bias_in), custom_call_target="tpu_custom_call" | custom-call | tf_op jit(solution)/shard_map/pallas_call | solution.py:443

commit v4 on v3

--- a/solution.py
+++ b/solution.py
@@ -48,14 +48,14 @@
 def step_kernel(count, groups, members, ids, weights, table_of, feats_in, shards, place_in, labels_in, top_in, bias_in, out_in,
                 logit_out, top_out, bias_out,
                 id_ref, weight_ref, table_ref, t_ref, place_ref, label_ref, w_ref, b_ref, o_ref, logit_ref, bias_ref,
-                load_sem, store_sem, code_ref, turned_ref, x_ref, fin_ref, xs_ref, ds_ref, key_ref, scale_ref, acc_ref, mine_ref,
-                got_ref, grad_ref, slope_ref, group_ref, half_ref, part_ref, bias_part,
+                load_sem, store_sem, code_ref, turned_ref, x_ref, fin_ref, xs_ref, ds_ref, key_ref, acc_ref, mine_ref, back_ref,
+                got_ref, grad_ref, slope_ref, group_ref, half_ref, send_ref, part_ref, bias_part,
                 x_send, x_recv, d_send, d_recv, s_send, s_recv, g_send, g_recv, p_send, p_recv,
                 b_send, b_recv, a_send, a_recv, f_send, f_recv, c_send, c_recv):
     my_g, my_t = lax.axis_index("grp"), lax.axis_index("tab")
     slots, vocab, width = t_ref.shape
     micro, local, columns = id_ref.shape
-    own = x_ref.shape[1] // 2
+    own = x_ref.shape[1]
     samples = x_ref.shape[2]
     hots = own // slots
     blocks = vocab // LANES
@@ -116,7 +116,7 @@
         (place_in, place_ref), (labels_in, label_ref), (top_in, w_ref), (bias_in, b_ref), (out_in, o_ref)))]
     for load in loads:
         load.start()
-    for load in loads[:3]:
+    for load in loads[:2]:
         load.wait()
 
     step = LANES // hots
@@ -126,30 +126,27 @@
         code = jnp.left_shift(LANES + (ids & (LANES - 1)), jnp.right_shift(ids, LANES.bit_length() - 1))
         code = code.astype(jnp.float32).astype(jnp.bfloat16)
         code_ref[c * step : (c + 1) * step] = code.T.astype(jnp.float32).reshape(step, hots, samples)
-        share = weight_ref[:, :, at].reshape(samples, LANES)
-        turned_ref[c * step : (c + 1) * step] = share.T.astype(jnp.float32).reshape(step, hots, samples)
 
     @pl.loop(0, members)
     def _(m):
-        held = [table_ref[m * slots + s] for s in range(slots)]
-        x_ref[m, 0:own] = jnp.concatenate([code_ref[t] for t in held], axis=0).astype(jnp.bfloat16)
-        x_ref[m, own : 2 * own] = jnp.concatenate([turned_ref[t] for t in held], axis=0).astype(jnp.bfloat16)
+        held = [code_ref[table_ref[m * slots + s]] for s in range(slots)]
+        x_ref[m] = jnp.concatenate(held, axis=0).astype(jnp.bfloat16)
 
     loads[3].wait()
     pl.semaphore_wait(barrier, members + groups - 2)
 
     def x_copy(k):
-        return remote(x_ref.at[member(k)], xs_ref.at[k], x_send.at[k], x_recv.at[k], my_g, member(k))
+        return remote(x_ref.at[member(k)], xs_ref.at[k], x_send, x_recv.at[k], my_g, member(k))
 
     def d_copy(k):
-        return remote(ds_ref.at[0], ds_ref.at[k], d_send.at[k], d_recv.at[k], my_g, member(k))
+        return remote(ds_ref.at[0], ds_ref.at[k], d_send, d_recv.at[k], my_g, member(k))
 
     def pass_copy(line, k):
         at = line * plane + k
-        return remote(ds_ref.at[line * plane], ds_ref.at[at], d_send.at[at], d_recv.at[at], my_g, member(k))
+        return remote(ds_ref.at[line * plane], ds_ref.at[at], d_send, d_recv.at[at], my_g, member(k))
 
     def s_copy(k):
-        return remote(mine_ref.at[k], got_ref.at[rows_of(my_t), :], s_send.at[k], s_recv.at[k], my_g, origin(k))
+        return remote(mine_ref.at[k], back_ref.at[k], s_send, s_recv.at[k], my_g, origin(k))
 
     @pl.loop(1, lines)
     def _(line):
@@ -159,18 +156,23 @@
     def _(k):
         d_copy(k).start()
 
-    for k in range(1, per):
+    @pl.loop(1, min(2 * per, members))
+    def _(k):
         x_copy(k).start()
 
-    @pl.loop(2 * per, members)
+    @pl.loop(3 * per, members)
     def _(k):
         x_copy(k).start()
 
-    @pl.loop(per, min(2 * per, members))
+    @pl.loop(2 * per, min(3 * per, members))
     def _(k):
         x_copy(k).start()
 
     xs_ref[0] = x_ref[my_t]
+    loads[2].wait()
+    for c in range(columns // LANES):
+        share = weight_ref[:, :, c * LANES : (c + 1) * LANES].reshape(samples, LANES)
+        turned_ref[c * step : (c + 1) * step] = share.T.astype(jnp.float32).reshape(step, hots, samples)
     loads[4].wait()
 
     parts = 2 if vocab % (2 * ROWS) == 0 else 1
@@ -180,17 +182,8 @@
 
     @pl.loop(0, turns)
     def _(turn):
-        @pl.when(turn == 1)
-        def _():
-            @pl.loop(1, lines)
-            def _(line):
-                d_copy(line * plane).wait_recv()
-
-                @pl.loop(1, plane)
-                def _(k):
-                    pass_copy(line, k).start()
-
-        i = lax.div(turn + turns - 2, turns - 1) * (1 + lax.rem(turn, turns - 1)) if turns > 1 else turn
+        late = lax.div(turn + turns - 2, turns)
+        i = (1 - late) * turn + late * (2 + lax.rem(turn - 1, turns - 2)) if turns > 2 else turn
 
         for e in range(per):
             @pl.when(lax.rem(per * i + e, plane) > 0)
@@ -202,13 +195,12 @@
                 x_copy(per * i + e).wait_recv()
 
         for e in range(per):
-            code = xs_ref[per * i + e, 0:own].astype(jnp.float32)
+            code = xs_ref[per * i + e].astype(jnp.float32)
             high = jnp.zeros(code.shape, jnp.int32)
             for k in range(1, blocks):
                 high = high + (code >= float(LANES << k)).astype(jnp.int32)
             low = jnp.right_shift(code.astype(jnp.int32), high) & (LANES - 1)
             key_ref[e] = high * LANES + low
-            scale_ref[e] = xs_ref[per * i + e, own : 2 * own].astype(jnp.float32)
 
         def look(slot):
             feats = ds_ref[pl.ds(per * i, per)].reshape(chunk, width)
@@ -225,30 +217,50 @@
                     p, r = divmod(v * ROWS, size)
                     return products[p][r : r + ROWS, e * samples : (e + 1) * samples]
 
-                got = choose_rows(tile_of, key & (ROWS - 1), bits, 0, tiles)
-                acc_ref[e, at, :] = got * scale_ref[e, at, :]
+                acc_ref[e, at, :] = choose_rows(tile_of, key & (ROWS - 1), bits, 0, tiles)
 
         @pl.loop(0, slots // unroll)
         def _(q):
+            line = turn * (slots // unroll) + q - max(slots // unroll, 2) + 2
+
+            @pl.when((line > 0) & (line < lines))
+            def _():
+                d_copy(line * plane).wait_recv()
+
+                @pl.loop(1, plane)
+                def _(k):
+                    pass_copy(line, k).start()
+
             for u in range(unroll):
                 look(q * unroll + u)
 
         for e in range(per):
-            total = jnp.sum(acc_ref[e].reshape(slots, hots, samples), axis=1)
-            mine_ref[per * i + e] = (total * (1.0 / math.sqrt(width))).astype(jnp.bfloat16).astype(jnp.float32)
+            mine_ref[per * i + e] = acc_ref[e].astype(jnp.bfloat16)
 
         for e in range(per):
             @pl.when(per * i + e > 0)
             def _():
                 s_copy(per * i + e).start()
 
-    got_ref[rows_of(my_t), :] = mine_ref[0]
-
-    @pl.loop(1, members)
-    def _(k):
-        d_copy(k).wait_send()
-        x_copy(k).wait_send()
-        s_copy(k).wait()
+    back_ref[0] = mine_ref[0]
+
+    @pl.loop(0, members)
+    def _(n):
+        k = lax.rem(n + 3 * per, members)
+
+        @pl.when(k > 0)
+        def _():
+            s_copy(k).wait_recv()
+
+        t = member(k)
+        shares = jnp.concatenate([turned_ref[table_ref[t * slots + s]] for s in range(slots)], axis=0)
+        total = jnp.sum((back_ref[k].astype(jnp.float32) * shares).reshape(slots, hots, samples), axis=1)
+        got_ref[rows_of(t), :] = (total * (1.0 / math.sqrt(width))).astype(jnp.bfloat16).astype(jnp.float32)
+
+    rest = pl.ds(1, members - 1)
+    remote(ds_ref.at[rest], ds_ref.at[rest], d_send, d_recv.at[0], my_g, my_t).wait_send()
+    remote(x_ref.at[rest], xs_ref.at[rest], x_send, x_recv.at[0], my_g, my_t).wait_send()
+    remote(mine_ref.at[rest], back_ref.at[rest], s_send, s_recv.at[0], my_g, my_t).wait_send()
 
     for load in loads[5:]:
         load.wait()
@@ -290,11 +302,13 @@
         g_copy(k).wait()
         half_ref[...] += group_ref[k]
 
+    send_ref[...] = half_ref[0:tables].reshape(members, slots, piece).astype(jnp.bfloat16)
+
     def p_copy(k):
-        return remote(half_ref.at[rows_of(member(k)), :], part_ref.at[k], p_send.at[k], p_recv.at[k], my_g, member(k))
+        return remote(send_ref.at[member(k)], part_ref.at[k], p_send, p_recv, my_g, member(k))
 
     def b_copy(k):
-        return remote(half_ref.at[pl.ds(tables, 1), :], bias_part.at[k], b_send.at[k], b_recv.at[k], my_g, member(k))
+        return remote(half_ref.at[pl.ds(tables, 1), :], bias_part.at[k], b_send, b_recv, my_g, member(k))
 
     @pl.loop(1, members)
     def _(k):
@@ -304,22 +318,22 @@
     def _(k):
         b_copy(k).start()
 
-    part_ref[0] = half_ref[rows_of(my_t), :]
     bias_part[0] = half_ref[tables : tables + 1, :]
 
-    @pl.loop(1, members)
-    def _(k):
-        p_copy(k).wait()
-
-    fin_ref[my_t, :, cols_of(my_g)] = jnp.sum(part_ref[...], axis=0).astype(jnp.bfloat16)
+    remote(send_ref.at[rest], part_ref.at[rest], p_send, p_recv, my_g, my_t).wait()
+
+    whole = half_ref[rows_of(my_t), :]
+    for k in range(1, members):
+        whole = whole + part_ref[k].astype(jnp.float32)
+    fin_ref[my_t, :, cols_of(my_g)] = whole.astype(jnp.bfloat16)
 
     def a_copy(k):
         at = fin_ref.at[my_t, :, cols_of(my_g)]
-        return remote(at, at, a_send.at[k], a_recv.at[k], my_g, member(k))
-
-    def f_copy(k, j):
-        at = fin_ref.at[origin(k), :, cols_of(my_g)]
-        return remote(at, at, f_send.at[j, k], f_recv.at[j, k], team(j), my_t)
+        return remote(at, at, a_send, a_recv, my_g, member(k))
+
+    def f_copy(j):
+        at = fin_ref.at[:, :, cols_of(my_g)]
+        return remote(at, at, f_send.at[j], f_recv.at[j], team(j), my_t)
 
     def c_copy(j):
         at = bias_ref.at[:, cols_of(my_g)]
@@ -329,16 +343,10 @@
     def _(k):
         a_copy(k).start()
 
-    @pl.loop(1, groups)
-    def _(j):
-        f_copy(0, j).start()
-
-    @pl.loop(1, members)
-    def _(k):
-        b_copy(k).wait()
+    remote(bias_part.at[rest], bias_part.at[rest], b_send, b_recv, my_g, my_t).wait()
 
     def add(q, total):
-        return total + bias_part[lax.rem(my_t - q + members, members)]
+        return total + bias_part[origin(q)]
 
     bias_ref[:, cols_of(my_g)] = lax.fori_loop(1, members, add, bias_part[my_t])
 
@@ -346,25 +354,17 @@
     def _(j):
         c_copy(j).start()
 
-    @pl.loop(1, members)
-    def _(k):
-        a_copy(k).wait_recv()
-
-        @pl.loop(1, groups)
-        def _(j):
-            f_copy(k, j).start()
-
-    @pl.loop(1, members)
-    def _(k):
-        a_copy(k).wait_send()
+    held = fin_ref.at[rest, :, cols_of(my_g)]
+    remote(held, held, a_send, a_recv, my_g, my_t).wait()
+
+    @pl.loop(1, groups)
+    def _(j):
+        f_copy(j).start()
 
     @pl.loop(1, groups)
     def _(j):
         c_copy(j).wait()
-
-        @pl.loop(0, members)
-        def _(k):
-            f_copy(k, j).wait()
+        f_copy(j).wait()
 
     stores = [pltpu.make_async_copy(fin_ref, top_out, store_sem.at[1]),
               pltpu.make_async_copy(bias_ref, bias_out, store_sem.at[2])]
@@ -419,24 +419,24 @@
             dma((3,)),
             pltpu.VMEM((tables, hots, samples), f32),
             pltpu.VMEM((tables, hots, samples), f32),
-            pltpu.VMEM((members, 2 * own, samples), bf16),
+            pltpu.VMEM((members, own, samples), bf16),
             pltpu.VMEM((members, slots, hidden), bf16),
-            pltpu.VMEM((members, 2 * own, samples), bf16),
+            pltpu.VMEM((members, own, samples), bf16),
             pltpu.VMEM((members, samples, width), bf16),
             pltpu.VMEM((per, own, samples), jnp.int32),
             pltpu.VMEM((per, own, samples), f32),
-            pltpu.VMEM((per, own, samples), f32),
-            pltpu.VMEM((members, slots, samples), f32),
+            pltpu.VMEM((members, own, samples), bf16),
+            pltpu.VMEM((members, own, samples), bf16),
             pltpu.VMEM((tables, samples), f32),
             pltpu.VMEM((tables + 8, hidden), f32),
             pltpu.VMEM((samples, hidden), bf16),
             pltpu.VMEM((groups, tables + 8, piece), f32),
             pltpu.VMEM((tables + 8, piece), f32),
-            pltpu.VMEM((members, slots, piece), f32),
+            pltpu.VMEM((members, slots, piece), bf16),
+            pltpu.VMEM((members, slots, piece), bf16),
             pltpu.VMEM((members, 1, piece), f32),
         ]
-        + [dma((members,))] * 6 + [dma((groups,))] * 2 + [dma((members,))] * 6
-        + [dma((groups, members))] * 2 + [dma((groups,))] * 2,
+        + [dma, dma((members,))] * 3 + [dma((groups,))] * 2 + [dma] * 6 + [dma((groups,))] * 4,
         compiler_params=pltpu.CompilerParams(collective_id=1, has_side_effects=True),
     )(ids, id_weights, slot_table, d, table, slot_table.reshape(1, -1), labels, weight, bias.reshape(1, -1),
       out.reshape(-1, LANES))

time: 57.8 us -> 51.7 us (0.89)
  Pallas kernels: 57 us -> 50.9 us
    pallas_call x1, Pallas kernels: 55.2 us -> 49.1 us  [fused_step(): pl.pallas_call(functools.partial(step_kernel, count, groups, members), ou...]
where the time goes in v4:
time: 51.7 us; the launch traced here: 51.5 us
  Pallas kernels  50.9 us (98%)
  between operations  0.64 us (1%)
    pallas_call x1, Pallas kernels, fused_step(): pl.pallas_call(functools.partial(step_kernel, count, groups, members), ou...  49.1 us
    pallas_call x1, Pallas kernels, fused_step(): pl.pallas_call(finish_kernel, out_shape=(jax.ShapeDtypeStruct(labels.shap...  1.78 us

profile of v4, /device:TPU:0, one launch (start us, length us, event | category | flops | bytes accessed | tf_op | source)
XLA Modules:
  0.0 51.5 jit_solution(15439426695472666466)
XLA Ops:
  0.6 49.1 %shard_map.112 = (f32[4,32]{1,0:T(4,128)}, bf16[16,8,1024]{2,1,0:T(8,128)(2,1)}, f32[1,1024]{1,0:T(1,128)}) custom-call(s32[4,32,1024]{2,1,0:T(8,128)} %ids.1, bf16[4,32,1024]{2,1,0:T(8,128)(2,1)} %weights.1, s32[128]{0:T(128)} %table_of.1, bf16[128,128]{1,0:T(8,128)(2,1)} %bitcast.5, bf16[8,1536,128]{2,1,0:T(8,128)(2,1)} %shards.1, s32[1,128]{1,0:T(1,128)} %bitcast.8, ...), custom_call_target="tpu_custom_call" | custom-call | tf_op jit(solution)/shard_map/pallas_call | solution.py:397
  49.8 1.8 %shard_map.113 = (f32[4,32]{1,0:T(4,128)}, f32[128,1024]{1,0:T(8,128)}, f32[1,1024]{1,0:T(1,128)}) custom-call(f32[4,32]{1,0:T(4,128)} %get-tuple-element.9.logit_in, bf16[16,8,1024]{2,1,0:T(8,128)(2,1)} %get-tuple-element.10.top_in, f32[1,1024]{1,0:T(1,128)} %get-tuple-element.11.bias_in), custom_call_target="tpu_custom_call" | custom-call | tf_op jit(solution)/shard_map/pallas_call | solution.py:443

commit v5 on v4

--- a/solution.py
+++ b/solution.py
@@ -48,7 +48,7 @@
 def step_kernel(count, groups, members, ids, weights, table_of, feats_in, shards, place_in, labels_in, top_in, bias_in, out_in,
                 logit_out, top_out, bias_out,
                 id_ref, weight_ref, table_ref, t_ref, place_ref, label_ref, w_ref, b_ref, o_ref, logit_ref, bias_ref,
-                load_sem, store_sem, code_ref, turned_ref, x_ref, fin_ref, xs_ref, ds_ref, key_ref, acc_ref, mine_ref, back_ref,
+                load_sem, store_sem, code_ref, turned_ref, x_ref, fin_ref, xs_ref, ds_ref, mine_ref, back_ref,
                 got_ref, grad_ref, slope_ref, group_ref, half_ref, send_ref, part_ref, bias_part,
                 x_send, x_recv, d_send, d_recv, s_send, s_recv, g_send, g_recv, p_send, p_recv,
                 b_send, b_recv, a_send, a_recv, f_send, f_recv, c_send, c_recv):
@@ -70,20 +70,25 @@
     lines = members // plane
     even = members & (members - 1) == 0
 
+    flips = [(1 << bit) * (1 - 2 * lax.rem(lax.div(my_t, 1 << bit), 2)) for bit in range(members.bit_length() - 1)]
+
     def move(k, way):
         if even:
-            spot = 0
-            for bit in range(members.bit_length() - 1):
-                spot = spot + lax.rem(lax.div(my_t, 1 << bit) + lax.div(k, 1 << bit), 2) * (1 << bit)
+            spot = my_t
+            for bit, flip in enumerate(flips):
+                if isinstance(k, int):
+                    spot = spot + flip if k & (1 << bit) else spot
+                else:
+                    spot = spot + flip * lax.rem(lax.div(k, 1 << bit), 2)
             return spot
         line = lax.rem(lax.div(my_t, plane) + way * lax.div(k, plane) + lines, lines)
         return line * plane + lax.rem(lax.rem(my_t, plane) + way * lax.rem(k, plane) + plane, plane)
 
     def member(k):
-        return move(jnp.int32(k), 1)
+        return move(k if even else jnp.int32(k), 1)
 
     def origin(k):
-        return move(jnp.int32(k), -1)
+        return move(k if even else jnp.int32(k), -1)
 
     def team(k):
         return lax.rem(my_g + k, groups)
@@ -101,20 +106,22 @@
     def cols_of(g):
         return pl.ds(pl.multiple_of(g * piece, LANES), piece)
 
-    barrier = pltpu.get_barrier_semaphore()
-
-    @pl.loop(1, members)
-    def _(k):
-        pl.semaphore_signal(barrier, inc=1, device_id={"grp": my_g, "tab": member(k)}, device_id_type=MESH)
-
-    @pl.loop(1, groups)
-    def _(k):
-        pl.semaphore_signal(barrier, inc=1, device_id={"grp": team(k), "tab": my_t}, device_id_type=MESH)
-
     loads = [pltpu.make_async_copy(src, dst, load_sem.at[n]) for n, (src, dst) in enumerate((
         (table_of, table_ref), (ids, id_ref), (weights, weight_ref), (feats_in, ds_ref.at[0]), (shards, t_ref),
         (place_in, place_ref), (labels_in, label_ref), (top_in, w_ref), (bias_in, b_ref), (out_in, o_ref)))]
-    for load in loads:
+    for load in loads[:2]:
+        load.start()
+
+    barrier = pltpu.get_barrier_semaphore()
+
+    for k in range(members - 1, 0, -1):
+        pl.semaphore_signal(barrier, inc=1, device_id={"grp": my_g, "tab": member(k)}, device_id_type=MESH)
+
+    @pl.loop(1, groups)
+    def _(k):
+        pl.semaphore_signal(barrier, inc=1, device_id={"grp": team(k), "tab": my_t}, device_id_type=MESH)
+
+    for load in loads[2:]:
         load.start()
     for load in loads[:2]:
         load.wait()
@@ -148,25 +155,23 @@
     def s_copy(k):
         return remote(mine_ref.at[k], back_ref.at[k], s_send, s_recv.at[k], my_g, origin(k))
 
-    @pl.loop(1, lines)
+    near = min(2 * plane, members)
+
+    def give(first, last):
+        @pl.loop(first, last)
+        def _(k):
+            d_copy(k).start()
+            x_copy(k).start()
+
+    give(1, per)
+
+    @pl.loop(2, lines)
     def _(line):
         d_copy(line * plane).start()
 
-    @pl.loop(1, plane)
-    def _(k):
-        d_copy(k).start()
-
-    @pl.loop(1, min(2 * per, members))
-    def _(k):
-        x_copy(k).start()
-
-    @pl.loop(3 * per, members)
-    def _(k):
-        x_copy(k).start()
-
-    @pl.loop(2 * per, min(3 * per, members))
-    def _(k):
-        x_copy(k).start()
+    give(per, min(2 * per, near))
+    give(min(3 * per, near), near)
+    give(min(2 * per, near), min(3 * per, near))
 
     xs_ref[0] = x_ref[my_t]
     loads[2].wait()
@@ -176,71 +181,78 @@
     loads[4].wait()
 
     parts = 2 if vocab % (2 * ROWS) == 0 else 1
-    unroll = 4 if slots % 4 == 0 else 1
-
     turns = members // per
-
-    @pl.loop(0, turns)
+    twin = 2 if slots % 2 == 0 else 1
+
+    def pass_line(line):
+        d_copy(line * plane).wait_recv()
+
+        @pl.loop(1, plane)
+        def _(k):
+            pass_copy(line, k).start()
+
+    def arrive(k):
+        @pl.when((k < near) | (lax.rem(k, plane) > 0))
+        def _():
+            d_copy(k).wait_recv()
+
+        x_copy(k).wait_recv()
+
+    def look(i, first, last):
+        feats = ds_ref[pl.ds(per * i, per)].reshape(chunk, width)
+        size = vocab // parts
+        for slot in range(first, last, twin):
+            products = [[lax.dot_general(t_ref[slot + u, p * size : (p + 1) * size, :], feats, NT,
+                                         preferred_element_type=jnp.float32) for p in range(parts)] for u in range(twin)]
+            at = slice(slot * hots, (slot + twin) * hots)
+            for e in range(per):
+                code = xs_ref[per * i + e, at].astype(jnp.float32)
+                high = jnp.zeros(code.shape, jnp.int32)
+                for k in range(1, blocks):
+                    high = high + (code >= float(LANES << k)).astype(jnp.int32)
+                low = jnp.right_shift(code.astype(jnp.int32), high) & (LANES - 1)
+                ids = high * LANES + low
+                got = []
+                for u in range(twin):
+                    key = ids[u * hots : (u + 1) * hots]
+                    tile = jnp.right_shift(key, ROWS.bit_length() - 1)
+                    bits = [(tile & (1 << b)) != 0 for b in range((tiles - 1).bit_length())]
+
+                    def tile_of(v, u=u, e=e):
+                        p, r = divmod(v * ROWS, size)
+                        return products[u][p][r : r + ROWS, e * samples : (e + 1) * samples]
+
+                    got.append(choose_rows(tile_of, key & (ROWS - 1), bits, 0, tiles))
+                mine_ref[per * i + e, at] = jnp.concatenate(got, axis=0).astype(jnp.bfloat16)
+
+    for k in range(1, per):
+        arrive(k)
+    middle = slots // 2 // twin * twin
+    look(0, 0, middle)
+    if lines > 2:
+        pass_line(2)
+
+    @pl.loop(near, members)
+    def _(k):
+        x_copy(k).start()
+
+    look(0, middle, slots)
+    for k in range(1, per):
+        s_copy(k).start()
+
+    @pl.loop(1, turns)
     def _(turn):
+        @pl.when(turn + 2 < lines)
+        def _():
+            pass_line(turn + 2)
+
         late = lax.div(turn + turns - 2, turns)
         i = (1 - late) * turn + late * (2 + lax.rem(turn - 1, turns - 2)) if turns > 2 else turn
-
         for e in range(per):
-            @pl.when(lax.rem(per * i + e, plane) > 0)
-            def _():
-                d_copy(per * i + e).wait_recv()
-
-            @pl.when(per * i + e > 0)
-            def _():
-                x_copy(per * i + e).wait_recv()
-
+            arrive(per * i + e)
+        look(i, 0, slots)
         for e in range(per):
-            code = xs_ref[per * i + e].astype(jnp.float32)
-            high = jnp.zeros(code.shape, jnp.int32)
-            for k in range(1, blocks):
-                high = high + (code >= float(LANES << k)).astype(jnp.int32)
-            low = jnp.right_shift(code.astype(jnp.int32), high) & (LANES - 1)
-            key_ref[e] = high * LANES + low
-
-        def look(slot):
-            feats = ds_ref[pl.ds(per * i, per)].reshape(chunk, width)
-            size = vocab // parts
-            products = [lax.dot_general(t_ref[slot, p * size : (p + 1) * size, :], feats, NT,
-                                        preferred_element_type=jnp.float32) for p in range(parts)]
-            at = pl.ds(pl.multiple_of(slot * hots, hots), hots)
-            for e in range(per):
-                key = key_ref[e, at, :]
-                high = jnp.right_shift(key, ROWS.bit_length() - 1)
-                bits = [(high & (1 << b)) != 0 for b in range((tiles - 1).bit_length())]
-
-                def tile_of(v, e=e):
-                    p, r = divmod(v * ROWS, size)
-                    return products[p][r : r + ROWS, e * samples : (e + 1) * samples]
-
-                acc_ref[e, at, :] = choose_rows(tile_of, key & (ROWS - 1), bits, 0, tiles)
-
-        @pl.loop(0, slots // unroll)
-        def _(q):
-            line = turn * (slots // unroll) + q - max(slots // unroll, 2) + 2
-
-            @pl.when((line > 0) & (line < lines))
-            def _():
-                d_copy(line * plane).wait_recv()
-
-                @pl.loop(1, plane)
-                def _(k):
-                    pass_copy(line, k).start()
-
-            for u in range(unroll):
-                look(q * unroll + u)
-
-        for e in range(per):
-            mine_ref[per * i + e] = acc_ref[e].astype(jnp.bfloat16)
-
-        for e in range(per):
-            @pl.when(per * i + e > 0)
-            def _():
-                s_copy(per * i + e).start()
+            s_copy(per * i + e).start()
 
     back_ref[0] = mine_ref[0]
 
@@ -283,19 +295,20 @@
     delta = (jax.nn.sigmoid(logit) - column_of(labels)) * (loss_scale / count)
     slope = gate * (1.0 + pre * (1.0 - gate))
     slope_ref[...] = (delta * out * slope).astype(jnp.bfloat16)
-    grad = slope_ref[...]
-    grad_ref[pl.ds(tables, 8), :] = jnp.broadcast_to(
-        jnp.sum(grad.astype(jnp.float32), axis=0, keepdims=True), (8, hidden))
-    grad_ref[pl.ds(0, tables), :] = jnp.dot(scores, grad, preferred_element_type=jnp.float32)
-
     def g_copy(k):
         return remote(grad_ref.at[:, cols_of(team(k))], group_ref.at[k], g_send.at[k], g_recv.at[k], team(k), my_t)
 
-    @pl.loop(1, groups)
-    def _(k):
+    def gradient(g, into, at):
+        grad = slope_ref[:, cols_of(g)]
+        into[pl.ds(tables, 8), at] = jnp.broadcast_to(
+            jnp.sum(grad.astype(jnp.float32), axis=0, keepdims=True), (8, piece))
+        into[pl.ds(0, tables), at] = jnp.dot(scores, grad, preferred_element_type=jnp.float32)
+
+    for k in range(1, groups):
+        gradient(team(k), grad_ref, cols_of(team(k)))
         g_copy(k).start()
 
-    half_ref[...] = grad_ref[:, cols_of(my_g)]
+    gradient(my_g, half_ref, pl.ds(0, piece))
 
     @pl.loop(1, groups)
     def _(k):
@@ -332,12 +345,15 @@
         return remote(at, at, a_send, a_recv, my_g, member(k))
 
     def f_copy(j):
-        at = fin_ref.at[:, :, cols_of(my_g)]
-        return remote(at, at, f_send.at[j], f_recv.at[j], team(j), my_t)
+        return remote(fin_ref.at[:, :, cols_of(my_g)], top_out.at[:, :, cols_of(my_g)], f_send.at[j], f_recv.at[j],
+                      team(j), my_t)
 
     def c_copy(j):
-        at = bias_ref.at[:, cols_of(my_g)]
-        return remote(at, at, c_send.at[j], c_recv.at[j], team(j), my_t)
+        return remote(bias_ref.at[:, cols_of(my_g)], bias_out.at[:, cols_of(my_g)], c_send.at[j], c_recv.at[j],
+                      team(j), my_t)
+
+    stores = [pltpu.make_async_copy(fin_ref.at[:, :, cols_of(my_g)], top_out.at[:, :, cols_of(my_g)], store_sem.at[1]),
+              pltpu.make_async_copy(bias_ref.at[:, cols_of(my_g)], bias_out.at[:, cols_of(my_g)], store_sem.at[2])]
 
     @pl.loop(1, members)
     def _(k):
@@ -350,26 +366,20 @@
 
     bias_ref[:, cols_of(my_g)] = lax.fori_loop(1, members, add, bias_part[my_t])
 
-    @pl.loop(1, groups)
-    def _(j):
+    for j in range(1, groups):
         c_copy(j).start()
+    stores[1].start()
 
     held = fin_ref.at[rest, :, cols_of(my_g)]
     remote(held, held, a_send, a_recv, my_g, my_t).wait()
 
-    @pl.loop(1, groups)
-    def _(j):
+    for j in range(1, groups):
         f_copy(j).start()
-
-    @pl.loop(1, groups)
-    def _(j):
+    stores[0].start()
+
+    for j in range(1, groups):
         c_copy(j).wait()
         f_copy(j).wait()
-
-    stores = [pltpu.make_async_copy(fin_ref, top_out, store_sem.at[1]),
-              pltpu.make_async_copy(bias_ref, bias_out, store_sem.at[2])]
-    for store in stores:
-        store.start()
     for store in [logit_store] + stores:
         store.wait()
 
@@ -423,8 +433,6 @@
             pltpu.VMEM((members, slots, hidden), bf16),
             pltpu.VMEM((members, own, samples), bf16),
             pltpu.VMEM((members, samples, width), bf16),
-            pltpu.VMEM((per, own, samples), jnp.int32),
-            pltpu.VMEM((per, own, samples), f32),
             pltpu.VMEM((members, own, samples), bf16),
             pltpu.VMEM((members, own, samples), bf16),
             pltpu.VMEM((tables, samples), f32),

time: 51.7 us -> 47.6 us (0.921)
  Pallas kernels: 50.9 us -> 46.8 us
    pallas_call x1, Pallas kernels: 49.1 us -> 45 us  [fused_step(): pl.pallas_call(functools.partial(step_kernel, count, groups, members), ou...]
where the time goes in v5:
time: 47.6 us; the launch traced here: 47.4 us
  Pallas kernels  46.8 us (98%)
  between operations  0.64 us (1%)
    pallas_call x1, Pallas kernels, fused_step(): pl.pallas_call(functools.partial(step_kernel, count, groups, members), ou...  45 us
    pallas_call x1, Pallas kernels, fused_step(): pl.pallas_call(finish_kernel, out_shape=(jax.ShapeDtypeStruct(labels.shap...  1.78 us

profile of v5, /device:TPU:0, one launch (start us, length us, event | category | flops | bytes accessed | tf_op | source)
XLA Modules:
  0.0 47.4 jit_solution(15659878670966373575)
XLA Ops:
  0.6 45.0 %shard_map.112 = (f32[4,32]{1,0:T(4,128)}, bf16[16,8,1024]{2,1,0:T(8,128)(2,1)}, f32[1,1024]{1,0:T(1,128)}) custom-call(s32[4,32,1024]{2,1,0:T(8,128)} %ids.1, bf16[4,32,1024]{2,1,0:T(8,128)(2,1)} %weights.1, s32[128]{0:T(128)} %table_of.1, bf16[128,128]{1,0:T(8,128)(2,1)} %bitcast.5, bf16[8,1536,128]{2,1,0:T(8,128)(2,1)} %shards.1, s32[1,128]{1,0:T(1,128)} %bitcast.8, ...), custom_call_target="tpu_custom_call" | custom-call | tf_op jit(solution)/shard_map/pallas_call | solution.py:407
  45.6 1.8 %shard_map.113 = (f32[4,32]{1,0:T(4,128)}, f32[128,1024]{1,0:T(8,128)}, f32[1,1024]{1,0:T(1,128)}) custom-call(f32[4,32]{1,0:T(4,128)} %get-tuple-element.9.logit_in, bf16[16,8,1024]{2,1,0:T(8,128)(2,1)} %get-tuple-element.10.top_in, f32[1,1024]{1,0:T(1,128)} %get-tuple-element.11.bias_in), custom_call_target="tpu_custom_call" | custom-call | tf_op jit(solution)/shard_map/pallas_call | solution.py:451

commit v6 on v5

--- a/solution.py
+++ b/solution.py
@@ -63,32 +63,24 @@
     tables = got_ref.shape[0]
     hidden = w_ref.shape[1]
     piece = hidden // groups
-    per = 2 if members % 2 == 0 else 1
-    chunk = per * samples
 
     plane = max(n for n in range(1, members + 1) if members % n == 0 and n * n <= members)
     lines = members // plane
-    even = members & (members - 1) == 0
-
     flips = [(1 << bit) * (1 - 2 * lax.rem(lax.div(my_t, 1 << bit), 2)) for bit in range(members.bit_length() - 1)]
 
-    def move(k, way):
-        if even:
-            spot = my_t
-            for bit, flip in enumerate(flips):
-                if isinstance(k, int):
-                    spot = spot + flip if k & (1 << bit) else spot
-                else:
-                    spot = spot + flip * lax.rem(lax.div(k, 1 << bit), 2)
-            return spot
-        line = lax.rem(lax.div(my_t, plane) + way * lax.div(k, plane) + lines, lines)
-        return line * plane + lax.rem(lax.rem(my_t, plane) + way * lax.rem(k, plane) + plane, plane)
-
     def member(k):
-        return move(k if even else jnp.int32(k), 1)
-
-    def origin(k):
-        return move(k if even else jnp.int32(k), -1)
+        spot = my_t
+        for bit, flip in enumerate(flips):
+            if isinstance(k, int):
+                spot = spot + flip if k & (1 << bit) else spot
+            else:
+                spot = spot + flip * lax.rem(lax.div(k, 1 << bit), 2)
+        return spot
+
+    def peer(j):
+        if isinstance(j, int):
+            return member(plane if j == members - 1 else j + (j >= plane))
+        return member(j + lax.div(j + members - plane, members) - (members - plane) * lax.div(j + 1, members))
 
     def team(k):
         return lax.rem(my_g + k, groups)
@@ -142,131 +134,144 @@
     loads[3].wait()
     pl.semaphore_wait(barrier, members + groups - 2)
 
-    def x_copy(k):
-        return remote(x_ref.at[member(k)], xs_ref.at[k], x_send, x_recv.at[k], my_g, member(k))
-
-    def d_copy(k):
-        return remote(ds_ref.at[0], ds_ref.at[k], d_send, d_recv.at[k], my_g, member(k))
+    def x_copy(j):
+        return remote(x_ref.at[peer(j)], xs_ref.at[j], x_send, x_recv.at[j], my_g, peer(j))
+
+    def d_copy(j):
+        return remote(ds_ref.at[0], ds_ref.at[j], d_send, d_recv.at[j], my_g, peer(j))
 
     def pass_copy(line, k):
-        at = line * plane + k
-        return remote(ds_ref.at[line * plane], ds_ref.at[at], d_send, d_recv.at[at], my_g, member(k))
-
-    def s_copy(k):
-        return remote(mine_ref.at[k], back_ref.at[k], s_send, s_recv.at[k], my_g, origin(k))
-
-    near = min(2 * plane, members)
-
-    def give(first, last):
-        @pl.loop(first, last)
-        def _(k):
-            d_copy(k).start()
-            x_copy(k).start()
-
-    give(1, per)
-
-    @pl.loop(2, lines)
-    def _(line):
-        d_copy(line * plane).start()
-
-    give(per, min(2 * per, near))
-    give(min(3 * per, near), near)
-    give(min(2 * per, near), min(3 * per, near))
+        at = line * plane + k - 1
+        return remote(ds_ref.at[line * plane - 1], ds_ref.at[at], d_send, d_recv.at[at], my_g, member(k))
+
+    def s_copy(j):
+        return remote(mine_ref.at[j], back_ref.at[j], s_send, s_recv.at[j], my_g, peer(j))
+
+    far = 2 * plane - 1
+    last = members - 1
+
+    def give(j):
+        d_copy(j).start()
+        x_copy(j).start()
+
+    give(1)
+    give(2)
+    for line in range(2, lines):
+        d_copy(line * plane - 1).start()
+    for j in range(3, far):
+        give(j)
+    give(last)
 
     xs_ref[0] = x_ref[my_t]
+    loads[4].wait()
+    parts = 2 if vocab % (2 * ROWS) == 0 else 1
+    size = vocab // parts
+    pairs = (members - 2) // 2
+
+    def pass_line(line):
+        d_copy(line * plane - 1).wait_recv()
+        for k in range(1, plane):
+            pass_copy(line, k).start()
+
+    def search(j, slot, tile_of):
+        at = slice(slot * hots, (slot + 2) * hots)
+        code = xs_ref[j, at].astype(jnp.float32)
+        high = jnp.zeros(code.shape, jnp.int32)
+        for k in range(1, blocks):
+            high = high + (code >= float(LANES << k)).astype(jnp.int32)
+        low = jnp.right_shift(code.astype(jnp.int32), high) & (LANES - 1)
+        ids = high * LANES + low
+        got = []
+        for u in range(2):
+            key = ids[u * hots : (u + 1) * hots]
+            tile = jnp.right_shift(key, ROWS.bit_length() - 1)
+            bits = [(tile & (1 << b)) != 0 for b in range((tiles - 1).bit_length())]
+            got.append(choose_rows(functools.partial(tile_of, u), key & (ROWS - 1), bits, 0, tiles))
+        mine_ref[j, at] = jnp.concatenate(got, axis=0).astype(jnp.bfloat16)
+
+    def span(p):
+        return slice(p * size, (p + 1) * size)
+
+    def look_pair(j, first, end):
+        feats = ds_ref[pl.ds(j, 2)].reshape(2 * samples, width)
+        for slot in range(first, end, 2):
+            products = [[lax.dot_general(t_ref[slot + u, span(p), :], feats, NT, preferred_element_type=jnp.float32)
+                         for p in range(parts)] for u in range(2)]
+            for e in range(2):
+                def tile_of(u, v):
+                    p, r = divmod(v * ROWS, size)
+                    return products[u][p][r : r + ROWS, e * samples : (e + 1) * samples]
+
+                search(j + e, slot, tile_of)
+
+    def look_one(j):
+        feats = ds_ref[j]
+        none = jnp.zeros_like(feats)
+        feats = jnp.concatenate([jnp.concatenate([feats, none], axis=1), jnp.concatenate([none, feats], axis=1)], axis=0)
+        for slot in range(0, slots, 2):
+            products = [lax.dot_general(jnp.concatenate([t_ref[slot, span(p), :], t_ref[slot + 1, span(p), :]], axis=1),
+                                        feats, NT, preferred_element_type=jnp.float32) for p in range(parts)]
+
+            def tile_of(u, v):
+                p, r = divmod(v * ROWS, size)
+                return products[p][r : r + ROWS, u * samples : (u + 1) * samples]
+
+            search(j, slot, tile_of)
+
+    look_one(0)
+    back_ref[0] = mine_ref[0]
     loads[2].wait()
     for c in range(columns // LANES):
         share = weight_ref[:, :, c * LANES : (c + 1) * LANES].reshape(samples, LANES)
         turned_ref[c * step : (c + 1) * step] = share.T.astype(jnp.float32).reshape(step, hots, samples)
-    loads[4].wait()
-
-    parts = 2 if vocab % (2 * ROWS) == 0 else 1
-    turns = members // per
-    twin = 2 if slots % 2 == 0 else 1
-
-    def pass_line(line):
-        d_copy(line * plane).wait_recv()
-
-        @pl.loop(1, plane)
-        def _(k):
-            pass_copy(line, k).start()
-
-    def arrive(k):
-        @pl.when((k < near) | (lax.rem(k, plane) > 0))
-        def _():
-            d_copy(k).wait_recv()
-
-        x_copy(k).wait_recv()
-
-    def look(i, first, last):
-        feats = ds_ref[pl.ds(per * i, per)].reshape(chunk, width)
-        size = vocab // parts
-        for slot in range(first, last, twin):
-            products = [[lax.dot_general(t_ref[slot + u, p * size : (p + 1) * size, :], feats, NT,
-                                         preferred_element_type=jnp.float32) for p in range(parts)] for u in range(twin)]
-            at = slice(slot * hots, (slot + twin) * hots)
-            for e in range(per):
-                code = xs_ref[per * i + e, at].astype(jnp.float32)
-                high = jnp.zeros(code.shape, jnp.int32)
-                for k in range(1, blocks):
-                    high = high + (code >= float(LANES << k)).astype(jnp.int32)
-                low = jnp.right_shift(code.astype(jnp.int32), high) & (LANES - 1)
-                ids = high * LANES + low
-                got = []
-                for u in range(twin):
-                    key = ids[u * hots : (u + 1) * hots]
-                    tile = jnp.right_shift(key, ROWS.bit_length() - 1)
-                    bits = [(tile & (1 << b)) != 0 for b in range((tiles - 1).bit_length())]
-
-                    def tile_of(v, u=u, e=e):
-                        p, r = divmod(v * ROWS, size)
-                        return products[u][p][r : r + ROWS, e * samples : (e + 1) * samples]
-
-                    got.append(choose_rows(tile_of, key & (ROWS - 1), bits, 0, tiles))
-                mine_ref[per * i + e, at] = jnp.concatenate(got, axis=0).astype(jnp.bfloat16)
-
-    for k in range(1, per):
-        arrive(k)
-    middle = slots // 2 // twin * twin
-    look(0, 0, middle)
+
+    for j in (1, 2):
+        d_copy(j).wait_recv()
+        x_copy(j).wait_recv()
+    middle = slots // 4 * 2
+    look_pair(1, 0, middle)
     if lines > 2:
         pass_line(2)
-
-    @pl.loop(near, members)
-    def _(k):
-        x_copy(k).start()
-
-    look(0, middle, slots)
-    for k in range(1, per):
-        s_copy(k).start()
-
-    @pl.loop(1, turns)
+    for j in range(far, last):
+        x_copy(j).start()
+    look_pair(1, middle, slots)
+    for j in (1, 2):
+        s_copy(j).start()
+
+    @pl.loop(1, pairs)
     def _(turn):
         @pl.when(turn + 2 < lines)
         def _():
-            pass_line(turn + 2)
-
-        late = lax.div(turn + turns - 2, turns)
-        i = (1 - late) * turn + late * (2 + lax.rem(turn - 1, turns - 2)) if turns > 2 else turn
-        for e in range(per):
-            arrive(per * i + e)
-        look(i, 0, slots)
-        for e in range(per):
-            s_copy(per * i + e).start()
-
-    back_ref[0] = mine_ref[0]
+            d_copy((turn + 2) * plane - 1).wait_recv()
+            for k in range(1, plane):
+                pass_copy(turn + 2, k).start()
+
+        for e in range(2):
+            j = 2 * turn + 1 + e
+
+            @pl.when((j < far) | (lax.rem(j + 1, plane) > 0))
+            def _():
+                d_copy(j).wait_recv()
+
+            x_copy(j).wait_recv()
+        look_pair(2 * turn + 1, 0, slots)
+        for e in range(2):
+            s_copy(2 * turn + 1 + e).start()
+
+    d_copy(last).wait_recv()
+    x_copy(last).wait_recv()
+    look_one(last)
+    s_copy(last).start()
 
     @pl.loop(0, members)
-    def _(n):
-        k = lax.rem(n + 3 * per, members)
-
-        @pl.when(k > 0)
+    def _(j):
+        @pl.when(j > 0)
         def _():
-            s_copy(k).wait_recv()
-
-        t = member(k)
+            s_copy(j).wait_recv()
+
+        t = peer(j)
         shares = jnp.concatenate([turned_ref[table_ref[t * slots + s]] for s in range(slots)], axis=0)
-        total = jnp.sum((back_ref[k].astype(jnp.float32) * shares).reshape(slots, hots, samples), axis=1)
+        total = jnp.sum((back_ref[j].astype(jnp.float32) * shares).reshape(slots, hots, samples), axis=1)
         got_ref[rows_of(t), :] = (total * (1.0 / math.sqrt(width))).astype(jnp.bfloat16).astype(jnp.float32)
 
     rest = pl.ds(1, members - 1)
@@ -323,12 +328,9 @@
     def b_copy(k):
         return remote(half_ref.at[pl.ds(tables, 1), :], bias_part.at[k], b_send, b_recv, my_g, member(k))
 
-    @pl.loop(1, members)
-    def _(k):
+    for k in range(last, 0, -1):
         p_copy(k).start()
-
-    @pl.loop(1, members)
-    def _(k):
+    for k in range(last, 0, -1):
         b_copy(k).start()
 
     bias_part[0] = half_ref[tables : tables + 1, :]
@@ -355,14 +357,13 @@
     stores = [pltpu.make_async_copy(fin_ref.at[:, :, cols_of(my_g)], top_out.at[:, :, cols_of(my_g)], store_sem.at[1]),
               pltpu.make_async_copy(bias_ref.at[:, cols_of(my_g)], bias_out.at[:, cols_of(my_g)], store_sem.at[2])]
 
-    @pl.loop(1, members)
-    def _(k):
+    for k in range(last, 0, -1):
         a_copy(k).start()
 
     remote(bias_part.at[rest], bias_part.at[rest], b_send, b_recv, my_g, my_t).wait()
 
     def add(q, total):
-        return total + bias_part[origin(q)]
+        return total + bias_part[member(q)]
 
     bias_ref[:, cols_of(my_g)] = lax.fori_loop(1, members, add, bias_part[my_t])
 
@@ -397,7 +398,6 @@
     slots, vocab, _ = table.shape
     tables, hidden = weight.shape
     piece = hidden // groups
-    per = 2 if members % 2 == 0 else 1
     hots = ids.shape[2] // tables
     own = slots * hots
     vmem = pl.BlockSpec(memory_space=pltpu.VMEM)

time: 47.6 us -> 45.6 us (0.958)
  Pallas kernels: 46.8 us -> 44.8 us
    pallas_call x1, Pallas kernels: 45 us -> 43 us  [fused_step(): pl.pallas_call(functools.partial(step_kernel, count, groups, members), ou...]
where the time goes in v6:
time: 45.6 us; the launch traced here: 45.4 us
  Pallas kernels  44.8 us (98%)
  between operations  0.64 us (1%)
    pallas_call x1, Pallas kernels, fused_step(): pl.pallas_call(functools.partial(step_kernel, count, groups, members), ou...  43 us
    pallas_call x1, Pallas kernels, fused_step(): pl.pallas_call(finish_kernel, out_shape=(jax.ShapeDtypeStruct(labels.shap...  1.78 us

profile of v6, /device:TPU:0, one launch (start us, length us, event | category | flops | bytes accessed | tf_op | source)
XLA Modules:
  0.0 45.4 jit_solution(7735197035992800468)
XLA Ops:
  0.6 43.0 %shard_map.112 = (f32[4,32]{1,0:T(4,128)}, bf16[16,8,1024]{2,1,0:T(8,128)(2,1)}, f32[1,1024]{1,0:T(1,128)}) custom-call(s32[4,32,1024]{2,1,0:T(8,128)} %ids.1, bf16[4,32,1024]{2,1,0:T(8,128)(2,1)} %weights.1, s32[128]{0:T(128)} %table_of.1, bf16[128,128]{1,0:T(8,128)(2,1)} %bitcast.5, bf16[8,1536,128]{2,1,0:T(8,128)(2,1)} %shards.1, s32[1,128]{1,0:T(1,128)} %bitcast.8, ...), custom_call_target="tpu_custom_call" | custom-call | tf_op jit(solution)/shard_map/pallas_call | solution.py:407
  43.6 1.8 %shard_map.113 = (f32[4,32]{1,0:T(4,128)}, f32[128,1024]{1,0:T(8,128)}, f32[1,1024]{1,0:T(1,128)}) custom-call(f32[4,32]{1,0:T(4,128)} %get-tuple-element.9.logit_in, bf16[16,8,1024]{2,1,0:T(8,128)(2,1)} %get-tuple-element.10.top_in, f32[1,1024]{1,0:T(1,128)} %get-tuple-element.11.bias_in), custom_call_target="tpu_custom_call" | custom-call | tf_op jit(solution)/shard_map/pallas_call | solution.py:451

commit v7 on v6

--- a/solution.py
+++ b/solution.py
@@ -135,7 +135,7 @@
     pl.semaphore_wait(barrier, members + groups - 2)
 
     def x_copy(j):
-        return remote(x_ref.at[peer(j)], xs_ref.at[j], x_send, x_recv.at[j], my_g, peer(j))
+        return remote(x_ref.at[peer(j)], xs_ref.at[j], x_send, x_recv.at[lax.div(j + 1, 2)], my_g, peer(j))
 
     def d_copy(j):
         return remote(ds_ref.at[0], ds_ref.at[j], d_send, d_recv.at[j], my_g, peer(j))
@@ -145,7 +145,7 @@
         return remote(ds_ref.at[line * plane - 1], ds_ref.at[at], d_send, d_recv.at[at], my_g, member(k))
 
     def s_copy(j):
-        return remote(mine_ref.at[j], back_ref.at[j], s_send, s_recv.at[j], my_g, peer(j))
+        return remote(mine_ref.at[j], back_ref.at[j], s_send, s_recv.at[lax.div(j + 1, 2)], my_g, peer(j))
 
     far = 2 * plane - 1
     last = members - 1
@@ -225,9 +225,17 @@
         share = weight_ref[:, :, c * LANES : (c + 1) * LANES].reshape(samples, LANES)
         turned_ref[c * step : (c + 1) * step] = share.T.astype(jnp.float32).reshape(step, hots, samples)
 
+    def pair_in(j):
+        two = pl.ds(j, 2)
+        remote(x_ref.at[two], xs_ref.at[two], x_send, x_recv.at[lax.div(j + 1, 2)], my_g, my_t).wait_recv()
+
+    def pair_back(j):
+        two = pl.ds(j, 2)
+        remote(mine_ref.at[two], back_ref.at[two], s_send, s_recv.at[lax.div(j + 1, 2)], my_g, my_t).wait_recv()
+
     for j in (1, 2):
         d_copy(j).wait_recv()
-        x_copy(j).wait_recv()
+    pair_in(1)
     middle = slots // 4 * 2
     look_pair(1, 0, middle)
     if lines > 2:
@@ -253,7 +261,7 @@
             def _():
                 d_copy(j).wait_recv()
 
-            x_copy(j).wait_recv()
+        pair_in(2 * turn + 1)
         look_pair(2 * turn + 1, 0, slots)
         for e in range(2):
             s_copy(2 * turn + 1 + e).start()
@@ -263,21 +271,24 @@
     look_one(last)
     s_copy(last).start()
 
-    @pl.loop(0, members)
-    def _(j):
-        @pl.when(j > 0)
-        def _():
-            s_copy(j).wait_recv()
-
+    def settle(j):
         t = peer(j)
         shares = jnp.concatenate([turned_ref[table_ref[t * slots + s]] for s in range(slots)], axis=0)
         total = jnp.sum((back_ref[j].astype(jnp.float32) * shares).reshape(slots, hots, samples), axis=1)
         got_ref[rows_of(t), :] = (total * (1.0 / math.sqrt(width))).astype(jnp.bfloat16).astype(jnp.float32)
 
+    settle(0)
+
+    @pl.loop(0, pairs)
+    def _(turn):
+        pair_back(2 * turn + 1)
+        for e in range(2):
+            settle(2 * turn + 1 + e)
+
+    s_copy(last).wait_recv()
+    settle(last)
+
     rest = pl.ds(1, members - 1)
-    remote(ds_ref.at[rest], ds_ref.at[rest], d_send, d_recv.at[0], my_g, my_t).wait_send()
-    remote(x_ref.at[rest], xs_ref.at[rest], x_send, x_recv.at[0], my_g, my_t).wait_send()
-    remote(mine_ref.at[rest], back_ref.at[rest], s_send, s_recv.at[0], my_g, my_t).wait_send()
 
     for load in loads[5:]:
         load.wait()
@@ -305,9 +316,10 @@
 
     def gradient(g, into, at):
         grad = slope_ref[:, cols_of(g)]
-        into[pl.ds(tables, 8), at] = jnp.broadcast_to(
-            jnp.sum(grad.astype(jnp.float32), axis=0, keepdims=True), (8, piece))
-        into[pl.ds(0, tables), at] = jnp.dot(scores, grad, preferred_element_type=jnp.float32)
+        side = into.shape[0] - tables
+        into[pl.ds(tables, side), at] = jnp.broadcast_to(
+            jnp.sum(grad.astype(jnp.float32), axis=0, keepdims=True), (side, piece)).astype(into.dtype)
+        into[pl.ds(0, tables), at] = jnp.dot(scores, grad, preferred_element_type=jnp.float32).astype(into.dtype)
 
     for k in range(1, groups):
         gradient(team(k), grad_ref, cols_of(team(k)))
@@ -315,10 +327,9 @@
 
     gradient(my_g, half_ref, pl.ds(0, piece))
 
-    @pl.loop(1, groups)
-    def _(k):
-        g_copy(k).wait()
-        half_ref[...] += group_ref[k]
+    for k in range(1, groups):
+        g_copy(k).wait_recv()
+        half_ref[...] += group_ref[k, 0 : tables + 8].astype(jnp.float32)
 
     send_ref[...] = half_ref[0:tables].reshape(members, slots, piece).astype(jnp.bfloat16)
 
@@ -335,7 +346,8 @@
 
     bias_part[0] = half_ref[tables : tables + 1, :]
 
-    remote(send_ref.at[rest], part_ref.at[rest], p_send, p_recv, my_g, my_t).wait()
+    parts_in = remote(send_ref.at[rest], part_ref.at[rest], p_send, p_recv, my_g, my_t)
+    parts_in.wait_recv()
 
     whole = half_ref[rows_of(my_t), :]
     for k in range(1, members):
@@ -360,7 +372,8 @@
     for k in range(last, 0, -1):
         a_copy(k).start()
 
-    remote(bias_part.at[rest], bias_part.at[rest], b_send, b_recv, my_g, my_t).wait()
+    sides_in = remote(bias_part.at[rest], bias_part.at[rest], b_send, b_recv, my_g, my_t)
+    sides_in.wait_recv()
 
     def add(q, total):
         return total + bias_part[member(q)]
@@ -372,12 +385,20 @@
     stores[1].start()
 
     held = fin_ref.at[rest, :, cols_of(my_g)]
-    remote(held, held, a_send, a_recv, my_g, my_t).wait()
+    rows_in = remote(held, held, a_send, a_recv, my_g, my_t)
+    rows_in.wait_recv()
 
     for j in range(1, groups):
         f_copy(j).start()
     stores[0].start()
 
+    remote(ds_ref.at[rest], ds_ref.at[rest], d_send, d_recv.at[0], my_g, my_t).wait_send()
+    remote(x_ref.at[rest], xs_ref.at[rest], x_send, x_recv.at[0], my_g, my_t).wait_send()
+    remote(mine_ref.at[rest], back_ref.at[rest], s_send, s_recv.at[0], my_g, my_t).wait_send()
+    for k in range(1, groups):
+        g_copy(k).wait_send()
+    for done in (parts_in, sides_in, rows_in):
+        done.wait_send()
     for j in range(1, groups):
         c_copy(j).wait()
         f_copy(j).wait()
@@ -436,15 +457,15 @@
             pltpu.VMEM((members, own, samples), bf16),
             pltpu.VMEM((members, own, samples), bf16),
             pltpu.VMEM((tables, samples), f32),
-            pltpu.VMEM((tables + 8, hidden), f32),
+            pltpu.VMEM((tables + 16, hidden), bf16),
             pltpu.VMEM((samples, hidden), bf16),
-            pltpu.VMEM((groups, tables + 8, piece), f32),
+            pltpu.VMEM((groups, tables + 16, piece), bf16),
             pltpu.VMEM((tables + 8, piece), f32),
             pltpu.VMEM((members, slots, piece), bf16),
             pltpu.VMEM((members, slots, piece), bf16),
             pltpu.VMEM((members, 1, piece), f32),
         ]
-        + [dma, dma((members,))] * 3 + [dma((groups,))] * 2 + [dma] * 6 + [dma((groups,))] * 4,
+        + [dma, dma((members // 2 + 1,)), dma, dma((members,)), dma, dma((members // 2 + 1,))] + [dma((groups,))] * 2 + [dma] * 6 + [dma((groups,))] * 4,
         compiler_params=pltpu.CompilerParams(collective_id=1, has_side_effects=True),
     )(ids, id_weights, slot_table, d, table, slot_table.reshape(1, -1), labels, weight, bias.reshape(1, -1),
       out.reshape(-1, LANES))

time: 45.6 us -> 45.2 us (level)
  no operation moved by 1% of the time
where the time goes in v7:
time: 45.2 us; the launch traced here: 45.1 us
  Pallas kernels  44.4 us (98%)
  between operations  0.64 us (1%)
    pallas_call x1, Pallas kernels, fused_step(): pl.pallas_call(functools.partial(step_kernel, count, groups, members), ou...  42.6 us
    pallas_call x1, Pallas kernels, fused_step(): pl.pallas_call(finish_kernel, out_shape=(jax.ShapeDtypeStruct(labels.shap...  1.78 us

profile of v7, /device:TPU:0, one launch (start us, length us, event | category | flops | bytes accessed | tf_op | source)
XLA Modules:
  0.0 45.1 jit_solution(463666097982345632)
XLA Ops:
  0.6 42.6 %shard_map.112 = (f32[4,32]{1,0:T(4,128)}, bf16[16,8,1024]{2,1,0:T(8,128)(2,1)}, f32[1,1024]{1,0:T(1,128)}) custom-call(s32[4,32,1024]{2,1,0:T(8,128)} %ids.1, bf16[4,32,1024]{2,1,0:T(8,128)(2,1)} %weights.1, s32[128]{0:T(128)} %table_of.1, bf16[128,128]{1,0:T(8,128)(2,1)} %bitcast.5, bf16[8,1536,128]{2,1,0:T(8,128)(2,1)} %shards.1, s32[1,128]{1,0:T(1,128)} %bitcast.8, ...), custom_call_target="tpu_custom_call" | custom-call | tf_op jit(solution)/shard_map/pallas_call | solution.py:428
  43.3 1.8 %shard_map.113 = (f32[4,32]{1,0:T(4,128)}, f32[128,1024]{1,0:T(8,128)}, f32[1,1024]{1,0:T(1,128)}) custom-call(f32[4,32]{1,0:T(4,128)} %get-tuple-element.9.logit_in, bf16[16,8,1024]{2,1,0:T(8,128)(2,1)} %get-tuple-element.10.top_in, f32[1,1024]{1,0:T(1,128)} %get-tuple-element.11.bias_in), custom_call_target="tpu_custom_call" | custom-call | tf_op jit(solution)/shard_map/pallas_call | solution.py:472

commit v8 on v7

--- a/solution.py
+++ b/solution.py
@@ -167,6 +167,11 @@
     parts = 2 if vocab % (2 * ROWS) == 0 else 1
     size = vocab // parts
     pairs = (members - 2) // 2
+    turned = plane - 1
+
+    def pair_of(turn):
+        late = lax.div(turn + pairs - turned, pairs)
+        return turn + late * (turned + lax.rem(turn + 1 - turned, pairs - turned) - turn)
 
     def pass_line(line):
         d_copy(line * plane - 1).wait_recv()
@@ -240,7 +245,7 @@
     look_pair(1, 0, middle)
     if lines > 2:
         pass_line(2)
-    for j in range(far, last):
+    for j in [*range(far + 2, last), far, far + 1]:
         x_copy(j).start()
     look_pair(1, middle, slots)
     for j in (1, 2):
@@ -254,17 +259,18 @@
             for k in range(1, plane):
                 pass_copy(turn + 2, k).start()
 
+        i = pair_of(turn)
         for e in range(2):
-            j = 2 * turn + 1 + e
+            j = 2 * i + 1 + e
 
             @pl.when((j < far) | (lax.rem(j + 1, plane) > 0))
             def _():
                 d_copy(j).wait_recv()
 
-        pair_in(2 * turn + 1)
-        look_pair(2 * turn + 1, 0, slots)
+        pair_in(2 * i + 1)
+        look_pair(2 * i + 1, 0, slots)
         for e in range(2):
-            s_copy(2 * turn + 1 + e).start()
+            s_copy(2 * i + 1 + e).start()
 
     d_copy(last).wait_recv()
     x_copy(last).wait_recv()
@@ -281,9 +287,10 @@
 
     @pl.loop(0, pairs)
     def _(turn):
-        pair_back(2 * turn + 1)
+        i = pair_of(turn)
+        pair_back(2 * i + 1)
         for e in range(2):
-            settle(2 * turn + 1 + e)
+            settle(2 * i + 1 + e)
 
     s_copy(last).wait_recv()
     settle(last)

time: 45.2 us -> 44.6 us (0.987)
  Pallas kernels: 44.4 us -> 43.8 us
    pallas_call x1, Pallas kernels: 42.6 us -> 42 us  [fused_step(): pl.pallas_call(functools.partial(step_kernel, count, groups, members), ou...]
where the time goes in v8:
time: 44.6 us; the launch traced here: 44.4 us
  Pallas kernels  43.8 us (98%)
  between operations  0.64 us (1%)
    pallas_call x1, Pallas kernels, fused_step(): pl.pallas_call(functools.partial(step_kernel, count, groups, members), ou...  42 us
    pallas_call x1, Pallas kernels, fused_step(): pl.pallas_call(finish_kernel, out_shape=(jax.ShapeDtypeStruct(labels.shap...  1.78 us

profile of v8, /device:TPU:0, one launch (start us, length us, event | category | flops | bytes accessed | tf_op | source)
XLA Modules:
  0.0 44.4 jit_solution(854817454923635965)
XLA Ops:
  0.6 42.0 %shard_map.112 = (f32[4,32]{1,0:T(4,128)}, bf16[16,8,1024]{2,1,0:T(8,128)(2,1)}, f32[1,1024]{1,0:T(1,128)}) custom-call(s32[4,32,1024]{2,1,0:T(8,128)} %ids.1, bf16[4,32,1024]{2,1,0:T(8,128)(2,1)} %weights.1, s32[128]{0:T(128)} %table_of.1, bf16[128,128]{1,0:T(8,128)(2,1)} %bitcast.5, bf16[8,1536,128]{2,1,0:T(8,128)(2,1)} %shards.1, s32[1,128]{1,0:T(1,128)} %bitcast.8, ...), custom_call_target="tpu_custom_call" | custom-call | tf_op jit(solution)/shard_map/pallas_call | solution.py:435
  42.6 1.8 %shard_map.113 = (f32[4,32]{1,0:T(4,128)}, f32[128,1024]{1,0:T(8,128)}, f32[1,1024]{1,0:T(1,128)}) custom-call(f32[4,32]{1,0:T(4,128)} %get-tuple-element.9.logit_in, bf16[16,8,1024]{2,1,0:T(8,128)(2,1)} %get-tuple-element.10.top_in, f32[1,1024]{1,0:T(1,128)} %get-tuple-element.11.bias_in), custom_call_target="tpu_custom_call" | custom-call | tf_op jit(solution)/shard_map/pallas_call | solution.py:479

commit v9 on v8

--- a/solution.py
+++ b/solution.py
@@ -113,6 +113,13 @@
     def _(k):
         pl.semaphore_signal(barrier, inc=1, device_id={"grp": team(k), "tab": my_t}, device_id_type=MESH)
 
+    last = members - 1
+    lend = groups % 2 == 0
+    odd = lax.rem(my_g, 2) if lend else 1
+    seat = members - odd
+    if lend:
+        pl.semaphore_signal(barrier, inc=1, device_id={"grp": my_g + 1 - 2 * odd, "tab": peer(last)}, device_id_type=MESH)
+
     for load in loads[2:]:
         load.start()
     for load in loads[:2]:
@@ -132,7 +139,7 @@
         x_ref[m] = jnp.concatenate(held, axis=0).astype(jnp.bfloat16)
 
     loads[3].wait()
-    pl.semaphore_wait(barrier, members + groups - 2)
+    pl.semaphore_wait(barrier, members + groups - 2 + lend)
 
     def x_copy(j):
         return remote(x_ref.at[peer(j)], xs_ref.at[j], x_send, x_recv.at[lax.div(j + 1, 2)], my_g, peer(j))
@@ -148,7 +155,6 @@
         return remote(mine_ref.at[j], back_ref.at[j], s_send, s_recv.at[lax.div(j + 1, 2)], my_g, peer(j))
 
     far = 2 * plane - 1
-    last = members - 1
 
     def give(j):
         d_copy(j).start()
@@ -160,7 +166,9 @@
         d_copy(line * plane - 1).start()
     for j in range(3, far):
         give(j)
-    give(last)
+    remote(ds_ref.at[0], ds_ref.at[seat], d_send, d_recv.at[seat], my_g + 1 - odd, peer(last)).start()
+    remote(x_ref.at[peer(last)], xs_ref.at[seat], x_send, x_recv.at[members // 2 + 1 - odd], my_g + 1 - odd,
+           peer(last)).start()
 
     xs_ref[0] = x_ref[my_t]
     loads[4].wait()
@@ -272,10 +280,21 @@
         for e in range(2):
             s_copy(2 * i + 1 + e).start()
 
-    d_copy(last).wait_recv()
-    x_copy(last).wait_recv()
-    look_one(last)
-    s_copy(last).start()
+    def extra(n):
+        j = members - n
+        remote(ds_ref.at[0], ds_ref.at[j], d_send, d_recv.at[j], my_g, my_t).wait_recv()
+        remote(x_ref.at[0], xs_ref.at[j], x_send, x_recv.at[members // 2 + 1 - n], my_g, my_t).wait_recv()
+        look_one(j)
+        remote(mine_ref.at[j], back_ref.at[last], s_send, s_recv.at[members // 2], my_g - 1 + n, peer(last)).start()
+
+    if lend:
+        @pl.when(odd == 1)
+        def _():
+            @pl.loop(0, 2)
+            def _(n):
+                extra(n)
+    else:
+        extra(1)
 
     def settle(j):
         t = peer(j)
@@ -401,7 +420,18 @@
 
     remote(ds_ref.at[rest], ds_ref.at[rest], d_send, d_recv.at[0], my_g, my_t).wait_send()
     remote(x_ref.at[rest], xs_ref.at[rest], x_send, x_recv.at[0], my_g, my_t).wait_send()
-    remote(mine_ref.at[rest], back_ref.at[rest], s_send, s_recv.at[0], my_g, my_t).wait_send()
+    if lend:
+        @pl.when(odd == 1)
+        def _():
+            both = pl.ds(1, members)
+            remote(mine_ref.at[both], mine_ref.at[both], s_send, s_recv.at[0], my_g, my_t).wait_send()
+
+        @pl.when(odd == 0)
+        def _():
+            most = pl.ds(1, members - 2)
+            remote(mine_ref.at[most], mine_ref.at[most], s_send, s_recv.at[0], my_g, my_t).wait_send()
+    else:
+        remote(mine_ref.at[rest], back_ref.at[rest], s_send, s_recv.at[0], my_g, my_t).wait_send()
     for k in range(1, groups):
         g_copy(k).wait_send()
     for done in (parts_in, sides_in, rows_in):
@@ -459,9 +489,9 @@
             pltpu.VMEM((tables, hots, samples), f32),
             pltpu.VMEM((members, own, samples), bf16),
             pltpu.VMEM((members, slots, hidden), bf16),
-            pltpu.VMEM((members, own, samples), bf16),
-            pltpu.VMEM((members, samples, width), bf16),
-            pltpu.VMEM((members, own, samples), bf16),
+            pltpu.VMEM((members + 1, own, samples), bf16),
+            pltpu.VMEM((members + 1, samples, width), bf16),
+            pltpu.VMEM((members + 1, own, samples), bf16),
             pltpu.VMEM((members, own, samples), bf16),
             pltpu.VMEM((tables, samples), f32),
             pltpu.VMEM((tables + 16, hidden), bf16),
@@ -472,7 +502,7 @@
             pltpu.VMEM((members, slots, piece), bf16),
             pltpu.VMEM((members, 1, piece), f32),
         ]
-        + [dma, dma((members // 2 + 1,)), dma, dma((members,)), dma, dma((members // 2 + 1,))] + [dma((groups,))] * 2 + [dma] * 6 + [dma((groups,))] * 4,
+        + [dma, dma((members // 2 + 2,)), dma, dma((members + 1,)), dma, dma((members // 2 + 1,))] + [dma((groups,))] * 2 + [dma] * 6 + [dma((groups,))] * 4,
         compiler_params=pltpu.CompilerParams(collective_id=1, has_side_effects=True),
     )(ids, id_weights, slot_table, d, table, slot_table.reshape(1, -1), labels, weight, bias.reshape(1, -1),
       out.reshape(-1, LANES))

time: 44.6 us -> 44.6 us (level)
  no operation moved by 1% of the time
where the time goes in v9:
time: 44.6 us; the launch traced here: 44.5 us
  Pallas kernels  43.8 us (98%)
  between operations  0.64 us (1%)
    pallas_call x1, Pallas kernels, fused_step(): pl.pallas_call(functools.partial(step_kernel, count, groups, members), ou...  42 us
    pallas_call x1, Pallas kernels, fused_step(): pl.pallas_call(finish_kernel, out_shape=(jax.ShapeDtypeStruct(labels.shap...  1.78 us

profile of v9, /device:TPU:0, one launch (start us, length us, event | category | flops | bytes accessed | tf_op | source)
XLA Modules:
  0.0 44.5 jit_solution(14154918146161796490)
XLA Ops:
  0.6 42.0 %shard_map.112 = (f32[4,32]{1,0:T(4,128)}, bf16[16,8,1024]{2,1,0:T(8,128)(2,1)}, f32[1,1024]{1,0:T(1,128)}) custom-call(s32[4,32,1024]{2,1,0:T(8,128)} %ids.1, bf16[4,32,1024]{2,1,0:T(8,128)(2,1)} %weights.1, s32[128]{0:T(128)} %table_of.1, bf16[128,128]{1,0:T(8,128)(2,1)} %bitcast.5, bf16[8,1536,128]{2,1,0:T(8,128)(2,1)} %shards.1, s32[1,128]{1,0:T(1,128)} %bitcast.8, ...), custom_call_target="tpu_custom_call" | custom-call | tf_op jit(solution)/shard_map/pallas_call | solution.py:465
  42.7 1.8 %shard_map.113 = (f32[4,32]{1,0:T(4,128)}, f32[128,1024]{1,0:T(8,128)}, f32[1,1024]{1,0:T(1,128)}) custom-call(f32[4,32]{1,0:T(4,128)} %get-tuple-element.9.logit_in, bf16[16,8,1024]{2,1,0:T(8,128)(2,1)} %get-tuple-element.10.top_in, f32[1,1024]{1,0:T(1,128)} %get-tuple-element.11.bias_in), custom_call_target="tpu_custom_call" | custom-call | tf_op jit(solution)/shard_map/pallas_call | solution.py:509
